TPU v7x, 128 devices: a whole 4x4x4 slice. The times are simulated.
128 devices in a mesh: rows: 8 (over x, core), cols: 16 (over y, z).
Axes of the slice: x: 4, y: 4, z: 4, core: 2. Of those that a mesh axis runs over, the one named last changes fastest.
Arguments:
- source_points: bfloat16 [262144, 128], P(('rows', 'cols')), may hold values from -3 to 3
- target_points: bfloat16 [262144, 128], P('cols'), may hold values from -3 to 3
- source_cluster: int32 [262144], P(('rows', 'cols')), may hold values from 0 to 8191, as said below
- target_cluster: int32 [262144], P('cols'), may hold values from 0 to 8191, as said below
- active_blocks: int32 [1024, 4], replicated, may hold values from 0 to 1023, as said below
- active_count: int32 [1024], replicated, may hold values from 1 to 4, as said below
- row_weight: float32 [262144], P(('rows', 'cols')), may hold values from -4 to 4
- col_weight: float32 [262144], P('cols'), may hold values from -4 to 4
Outputs:
- row_potential: float32 [262144], P(('rows', 'cols'))
- col_potential: float32 [262144], P('cols')
- row_adjoint: float32 [262144], P(('rows', 'cols'))
- col_adjoint: float32 [262144], P('cols')
Inputs may be any that keep to these rules, and one draw needn't show every extreme that they name: `source_cluster`: never falling; the 2048 points of device d (its index along rows+cols) form clusters 64 * d to 64 * (d + 1) - 1, each of one point or more. `target_cluster`: never falling; the 16384 points of index c of cols form clusters 512 * c to 512 * (c + 1) - 1, each of one point or more. `active_blocks`: each row of 4 distinct column blocks lies within the 64 column blocks of one index of cols; the 8 row blocks of one device name pairwise different indices of cols; every column block is the first entry of exactly one row. Only the first active_count[q] entries of row q of active_blocks are active.
All inputs are finite; a program needn't handle non-finite values.
Results may differ from a plain program's by a relative error of at most 0.0003.
Values may be sent and summed in bfloat16 or wider, within the bound.
No kernel may reach another device: no remote copies, remote signals or barrier semaphores. Data moves between devices by JAX's collectives and lax.ppermute only.
A program may use at most 128 MiB of HBM per device.

v0:
```python
import jax
import jax.numpy as jnp
from jax import lax
from jax.experimental import pallas as pl
from jax.experimental.pallas import tpu as pltpu
from jax.sharding import Mesh
from jax.sharding import PartitionSpec as P


D = 128
BLOCK = 256
ACT = 4
ITER_C = 4
CL_DEV = 64
RBD = 8
CBD = 64
ROWS = ("x", "core")
COLS = ("y", "z")
ALL = ("x", "core", "y", "z")
N_ROWS = 8
N_COLS = 16
N_SRC = CL_DEV * N_COLS
N_TGT = 512
PTS_SRC = 2048
WINDOW = 136
PIECE = 32
PACKED = BLOCK + 16

SCALE = 2.8853900817779268
lowest = -1.0e30
HI = lax.Precision.HIGHEST
NT = (((1,), (1,)), ((), ()))

VM = pl.BlockSpec(memory_space=pltpu.VMEM)
SM = pl.BlockSpec(memory_space=pltpu.SMEM)
ANY = pl.BlockSpec(memory_space=pl.ANY)


def vmem_shape(*dims, dtype=jnp.float32):
    return pltpu.VMEM(dims, dtype)


def in_vmem(x):
    return pltpu.with_memory_space_constraint(x, pltpu.VMEM)


def in_hbm(x):
    return pltpu.with_memory_space_constraint(x, pltpu.HBM)


def eye(rows, shift=0):
    return lax.broadcasted_iota(jnp.int32, (rows, 128), 0) + shift == lax.broadcasted_iota(
        jnp.int32, (rows, 128), 1
    )


def to_row(column, mask):
    return jnp.sum(jnp.where(mask, column, 0.0), axis=0, keepdims=True)


def to_column(row, mask):
    return jnp.sum(jnp.where(mask, row, 0.0), axis=1, keepdims=True)


def lse_list(parts):
    highest = parts[0]
    for part in parts[1:]:
        highest = jnp.maximum(highest, part)
    terms = [jnp.exp2(part - highest) for part in parts]
    while len(terms) > 1:
        terms = [terms[k] + terms[k + 1] for k in range(0, len(terms), 2)]
    return highest + jnp.log2(terms[0])


def one_hot(labels, rows):
    hit = lax.broadcasted_iota(jnp.int32, (rows, labels.shape[1]), 0) == labels
    return jnp.where(hit, 1.0, 0.0).astype(jnp.bfloat16)


def totals_and_counts(hits, points):
    both = jnp.concatenate([points, jnp.ones(points.shape, jnp.bfloat16)], axis=1)
    return jnp.dot(hits, both, preferred_element_type=jnp.float32)


def source_means_kernel(base, points, labels, out):
    both = totals_and_counts(one_hot(labels[...] - base[0], CL_DEV), points[...])
    counts = both[:, D:]
    means = both[:, :D] / counts
    low = to_row(counts, eye(CL_DEV))
    high = to_row(counts, eye(CL_DEV, 64))
    tail = lax.broadcasted_iota(jnp.int32, (8, 128), 0)
    tail = jnp.where(tail == 0, low, jnp.where(tail == 1, high, 0.0))
    for peer in range(N_COLS):
        out[peer, :CL_DEV, :] = means
        out[peer, CL_DEV:, :] = tail


def target_means_kernel(base, firsts, points, labels, means, logs, acc):
    step = pl.program_id(0)

    @pl.when(step == 0)
    def _():
        acc[...] = jnp.zeros_like(acc)

    def piece(chunk, start, points_here):
        at = slice(chunk * 256, (chunk + 1) * 256)
        hits = one_hot(labels[0, :, at] - (start + base[0]), PIECE)
        window = pl.ds(pl.multiple_of(start, 8), PIECE)
        acc[window, :] += totals_and_counts(hits, points_here)

    starts, extra = [], []
    for chunk in range(8):
        index = 2 * (step * 8 + chunk)
        start = firsts[index] // 8 * 8
        beyond = jnp.where(index + 2 < 128, firsts[jnp.minimum(index + 2, 127)], N_TGT - 1)
        starts.append(start)
        extra.append((beyond - start) // PIECE)
        piece(chunk, start, points[chunk * 256 : (chunk + 1) * 256, :])
    for chunk in range(8):
        def more(k, carry, chunk=chunk):
            piece(chunk, starts[chunk] + k * PIECE, points[chunk * 256 : (chunk + 1) * 256, :])
            return carry

        lax.fori_loop(1, extra[chunk] + 1, more, 0)

    @pl.when(step == pl.num_programs(0) - 1)
    def _():
        mask = eye(128)
        for part in range(4):
            at = slice(part * 128, (part + 1) * 128)
            counts = acc[at, D:]
            means[at, :] = acc[at, :D] / counts
            logs[:, at] = jnp.log2(to_row(counts, mask))


def row_lse_chunk(scores):
    highest = jnp.max(scores, axis=1, keepdims=True)
    return highest + jnp.log2(jnp.sum(jnp.exp2(scores - highest), axis=1, keepdims=True))


def coarse_start_kernel(gathered, targets, gains, source_logs, out):
    mask = eye(128)
    y = targets[...]
    half_y = 0.5 * jnp.sum(y * y, axis=1, keepdims=True)
    half_y = jnp.concatenate(
        [to_row(half_y[k * 128 : (k + 1) * 128], mask) for k in range(4)], axis=1
    )
    for part in range(8):
        x = jnp.concatenate(
            [gathered[2 * part, :CL_DEV, :], gathered[2 * part + 1, :CL_DEV, :]], axis=0
        )
        counts = gathered[2 * part, 64:65, :] + gathered[2 * part + 1, 65:66, :]
        source_logs[part : part + 1, :] = jnp.log2(counts)
        half_x = 0.5 * jnp.sum(x * x, axis=1, keepdims=True)
        products = lax.dot_general(x, y, NT, precision=HI, preferred_element_type=jnp.float32)
        gain = SCALE * (products - (half_x + half_y))
        gains[part * 128 : (part + 1) * 128, :] = gain
        out[0, part : part + 1, :] = to_row(row_lse_chunk(gain), mask)
    first = out[0]
    for peer in range(1, N_COLS):
        out[peer] = first


def parts_of(refs):
    if len(refs) == 1:
        return [refs[0][k] for k in range(refs[0].shape[0])]
    return [ref[...] for ref in refs]


def coarse_rows_kernel(*refs):
    *gathered, target_logs, gains, out = refs
    mask = eye(128)
    potential = target_logs[...] - lse_list(parts_of(gathered))
    for part in range(8):
        pieces = []
        for piece in range(2):
            at = part * 128 + piece * 64
            pieces.append(row_lse_chunk(gains[at : at + 64, :] + potential))
        out[0, part : part + 1, :] = to_row(jnp.concatenate(pieces, axis=0), mask)
    first = out[0]
    for peer in range(1, N_COLS):
        out[peer] = first


def coarse_cols_kernel(*refs):
    *gathered, source_logs, gains, out, scores = refs
    mask = eye(128)
    potential = source_logs[...] - lse_list(parts_of(gathered))
    highest = jnp.full((8, N_TGT), lowest, jnp.float32)
    for part in range(8):
        at = slice(part * 128, (part + 1) * 128)
        value = gains[at, :] + to_column(potential[part : part + 1, :], mask)
        scores[at, :] = value
        highest = jnp.maximum(highest, jnp.max(value.reshape(16, 8, N_TGT), axis=0))
    highest = jnp.max(highest, axis=0, keepdims=True)
    total = jnp.zeros((8, N_TGT), jnp.float32)
    for part in range(8):
        at = slice(part * 128, (part + 1) * 128)
        value = jnp.exp2(scores[at, :] - highest)
        total = total + jnp.sum(value.reshape(16, 8, N_TGT), axis=0)
    result = highest + jnp.log2(jnp.sum(total, axis=0, keepdims=True))
    if len(out.shape) == 2:
        out[...] = result
    else:
        for peer in range(N_ROWS):
            out[peer] = result


def start_copies(counts, blocks, x_hbm, y_hbm, xs, ys, sems):
    def copies(slot):
        found = [pltpu.make_async_copy(x_hbm.at[slot], xs.at[slot], sems.at[slot, ACT])]
        for a in range(ACT):
            first = pl.multiple_of(blocks[slot * ACT + a] * BLOCK, BLOCK)
            found.append(
                pltpu.make_async_copy(
                    y_hbm.at[pl.ds(first, BLOCK), :], ys.at[slot * ACT + a], sems.at[slot, a]
                )
            )
        return found

    def begin(slot, carry):
        @pl.when(counts[slot] > 0)
        def _():
            for copy in copies(slot):
                copy.start()

        return carry

    lax.fori_loop(0, N_COLS, begin, 0)
    return copies


def half_norms_kernel(points, out):
    left = jnp.full((8, 2 * D), 1.0, jnp.bfloat16)
    for b in range(8):
        wide = points[b * BLOCK : (b + 1) * BLOCK, :].astype(jnp.float32)
        square = wide * wide
        high = square.astype(jnp.bfloat16)
        low = (square - high.astype(jnp.float32)).astype(jnp.bfloat16)
        right = jnp.concatenate([high, low], axis=1)
        total = lax.dot_general(left, right, NT, preferred_element_type=jnp.float32)
        out[b] = (0.5 * SCALE) * total[:1]


def products_kernel(counts, blocks, norms, x_hbm, y_hbm, gains, halves, weights, xs, ys, sems):
    copies = start_copies(counts, blocks, x_hbm, y_hbm, xs, ys, sems)
    mask = eye(128)

    def body(slot):
        x = xs[slot, :BLOCK, :]
        tail = xs[slot, BLOCK:, :].astype(jnp.float32)
        for h in range(2):
            at = slice(h * 128, (h + 1) * 128)
            wide = xs[slot, at, :].astype(jnp.float32)
            half_x = 0.5 * jnp.sum(wide * wide, axis=1, keepdims=True)
            halves[slot, :, at] = to_row(half_x, mask)
            weights[slot, :, at] = (tail[h : h + 1] + tail[h + 2 : h + 3]) + tail[h + 4 : h + 5]
        for a in range(ACT):
            products = lax.dot_general(
                x, ys[slot * ACT + a], NT, preferred_element_type=jnp.float32
            )
            gains[slot, :, a * BLOCK : (a + 1) * BLOCK] = (
                SCALE * products - norms[blocks[slot * ACT + a]]
            )

    each_slot(counts, body, copies)


def slot_potential(slot, counts, blocks, values):
    rows = []
    for a in range(ACT):
        row = values[blocks[slot * ACT + a]]
        rows.append(jnp.where(a < counts[slot], row, lowest))
    return jnp.concatenate(rows, axis=1)


CHUNK = 16
CHUNKS = BLOCK // CHUNK
WIDTH = ACT * BLOCK


def fine_slot(slot, counts, blocks, gains, work, values, best, weights=None, mixed=None, lam_out=None):
    potential = slot_potential(slot, counts, blocks, values)
    mask = eye(128)
    highest = jnp.full((8, WIDTH), lowest, jnp.float32)
    lams = []
    for k in range(CHUNKS):
        at = slice(k * CHUNK, (k + 1) * CHUNK)
        scores = gains[slot, at, :] + potential
        lam = row_lse_chunk(scores)
        scores = scores - lam
        work[at, :] = scores
        highest = jnp.maximum(highest, jnp.max(scores.reshape(CHUNK // 8, 8, WIDTH), axis=0))
        lams.append(lam)
    highest = jnp.max(highest, axis=0, keepdims=True)
    total = jnp.zeros((8, WIDTH), jnp.float32)
    if weights is not None:
        w_row = weights[slot]
        w_cols = [to_column(w_row[:, h * 128 : (h + 1) * 128], mask) for h in range(2)]
        w_col = jnp.concatenate(w_cols, axis=0)
        weighted = jnp.zeros((8, WIDTH), jnp.float32)
    for k in range(CHUNKS):
        at = slice(k * CHUNK, (k + 1) * CHUNK)
        value = jnp.exp2(work[at, :] - highest)
        total = total + jnp.sum(value.reshape(CHUNK // 8, 8, WIDTH), axis=0)
        if weights is not None:
            value = value * w_col[at]
            weighted = weighted + jnp.sum(value.reshape(CHUNK // 8, 8, WIDTH), axis=0)
    total = jnp.sum(total, axis=0, keepdims=True)
    result = highest + jnp.log2(total)
    if weights is not None:
        mean = jnp.sum(weighted, axis=0, keepdims=True) / total
    for a in range(ACT):
        block = blocks[slot * ACT + a]
        at = slice(a * BLOCK, (a + 1) * BLOCK)
        here = jnp.where(a < counts[slot], result[:, at] - values[block], lowest)
        old = best[block]
        top = jnp.maximum(old, here)
        old_part, new_part = jnp.exp2(old - top), jnp.exp2(here - top)
        both = old_part + new_part
        best[block] = top + jnp.log2(both)
        if weights is not None:
            mixed[block] = (mixed[block] * old_part + mean[:, at] * new_part) / both
    if lam_out is not None:
        for h in range(2):
            at = slice(h * 128, (h + 1) * 128)
            lam_out[slot, :, at] = to_row(jnp.concatenate(lams[h * 8 : (h + 1) * 8], axis=0), mask)


def clear(best, mixed=None):
    best[...] = jnp.full(best.shape, lowest, jnp.float32)
    if mixed is not None:
        mixed[...] = jnp.zeros(mixed.shape, jnp.float32)


def each_slot(counts, body, copies=None):
    def step(slot, carry):
        @pl.when(counts[slot] > 0)
        def _():
            if copies is not None:
                for copy in copies(slot):
                    copy.wait()
            body(slot)

        return carry

    lax.fori_loop(0, N_COLS, step, 0)


def first_pass_kernel(
    base, counts, blocks, starts, p0, p1, p2, p3, labels, gains, best, kept, values, table, work
):
    clear(best)
    mask = eye(128)
    cluster_values = -lse_list([p0[...], p1[...], p2[...], p3[...]])
    for part in range(4):
        at = slice(part * 128, (part + 1) * 128)
        table[at, :] = jnp.broadcast_to(to_column(cluster_values[:, at], mask), (128, 128))

    def spread(step, carry):
        for n in range(8):
            block, h = step * 4 + n // 2, n % 2
            first = starts[2 * block + h] // 8 * 8
            first = pl.multiple_of(jnp.minimum(first, N_TGT - WINDOW), 8)
            at = slice(h * 128, (h + 1) * 128)
            index = lax.broadcasted_iota(jnp.int32, (WINDOW, 128), 0)
            hit = index == labels[block, :, at] - (base[0] + first)
            window = table[pl.ds(first, WINDOW), :]
            values[block, :, at] = jnp.sum(jnp.where(hit, window, 0.0), axis=0, keepdims=True)
        return carry

    lax.fori_loop(0, CBD // 4, spread, 0)
    each_slot(
        counts, lambda slot: fine_slot(slot, counts, blocks, gains, work, values, best)
    )


def second_pass_kernel(
    counts, blocks, l0, l1, l2, l3, weights, gains, both, lam, kept, values, work
):
    best, mixed = both.at[:CBD], both.at[CBD:]
    clear(best, mixed)
    values[...] = -lse_list([l0[...], l1[...], l2[...], l3[...]])
    each_slot(
        counts,
        lambda slot: fine_slot(
            slot, counts, blocks, gains, work, values, best, weights, mixed, lam
        ),
    )


def adjoint_kernel(
    counts, blocks, b0, b1, b2, b3, lam, halves, weights, col_weights, gains,
    potential_out, adjoint_out, back, values,
):
    parts = [b0, b1, b2, b3]
    total = lse_list([part[:CBD] for part in parts])
    mixed = [part[CBD:] * jnp.exp2(part[:CBD] - total) for part in parts]
    mixed = (mixed[0] + mixed[1]) + (mixed[2] + mixed[3])
    values[...] = -total
    potential_out[...] = total * (-1.0 / SCALE)
    adjoint_out[...] = mixed + col_weights[...]
    back[...] = jnp.zeros(back.shape, jnp.float32)
    mask = eye(128)

    def body(slot):
        potential = slot_potential(slot, counts, blocks, values)
        spread = jnp.concatenate(
            [col_weights[blocks[slot * ACT + a]] for a in range(ACT)], axis=1
        )
        for h in range(2):
            half = slice(h * 128, (h + 1) * 128)
            shift = to_column(lam[slot, :, half], mask)
            sums, crossed = [], []
            for k in range(128 // CHUNK):
                at = slice(h * 128 + k * CHUNK, h * 128 + (k + 1) * CHUNK)
                scores = gains[slot, at, :] + potential
                entries = jnp.exp2(scores - shift[k * CHUNK : (k + 1) * CHUNK])
                sums.append(jnp.sum(entries, axis=1, keepdims=True))
                crossed.append(jnp.sum(entries * spread, axis=1, keepdims=True))
            mass = to_row(jnp.concatenate(sums, axis=0), mask)
            cross = to_row(jnp.concatenate(crossed, axis=0), mask)
            back[slot, :, half] = halves[slot, :, half] - lam[slot, :, half] * (1.0 / SCALE)
            back[slot, :, BLOCK + h * 128 : BLOCK + (h + 1) * 128] = (
                weights[slot, :, half] * mass + cross
            )

    each_slot(counts, body)


def spread_kernel(owners, points, weights, out):
    for q in range(RBD):
        owner = owners[q] // CBD
        out[owner, :BLOCK, :] = points[q * BLOCK : (q + 1) * BLOCK, :]
        rest = weights[q]
        pieces = []
        for _ in range(3):
            piece = rest.astype(jnp.bfloat16)
            rest = rest - piece.astype(jnp.float32)
            pieces.append(piece.astype(jnp.float32))
        pieces.append(jnp.zeros((10, D), jnp.float32))
        out[owner, BLOCK:, :] = jnp.concatenate(pieces, axis=0).astype(jnp.bfloat16)


def cost(flops):
    return pl.CostEstimate(flops=int(flops), transcendentals=0, bytes_accessed=4 << 20)


def call(kernel, out_shape, in_specs, scratch=(), flops=1e8, **kw):
    out_specs = jax.tree.map(lambda _: VM, out_shape, is_leaf=lambda x: hasattr(x, "shape"))
    return pl.pallas_call(
        kernel,
        out_shape=out_shape,
        in_specs=in_specs,
        out_specs=out_specs,
        scratch_shapes=list(scratch),
        compiler_params=pltpu.CompilerParams(vmem_limit_bytes=24 << 20),
        cost_estimate=cost(flops),
        **kw,
    )


def exchange(x, axis):
    return lax.all_to_all(x, axis, split_axis=0, concat_axis=0, tiled=True)


def partner(x, axis, step):
    n = lax.axis_size(axis)
    return lax.ppermute(x, axis, [(k, k ^ step) for k in range(n)])


def four_along(x, axis):
    found = [x]
    for step in (1, 2, 3):
        found.append(partner(x, axis, step))
    return found


def four_along_x(x):
    return [in_vmem(part) for part in four_along(x, "x")]


def on_device(
    source_points,
    target_points,
    source_cluster,
    target_cluster,
    active_blocks,
    active_count,
    row_weight,
    col_weight,
):
    row_index = lax.axis_index(ROWS)
    col_index = lax.axis_index(COLS)
    device = row_index * N_COLS + col_index

    source_base = (CL_DEV * device).reshape(1).astype(jnp.int32)
    target_base = (N_TGT * col_index).reshape(1).astype(jnp.int32)
    packed = call(
        source_means_kernel, vmem_shape(N_COLS, CL_DEV + 8, D), [SM, VM, VM]
    )(source_base, in_hbm(source_points), in_hbm(source_cluster.reshape(1, PTS_SRC)))
    gathered = exchange(packed, COLS)

    row_weights = row_weight.reshape(RBD, 2, 128)
    col_weights = col_weight.reshape(CBD, 1, BLOCK)
    first_blocks = lax.dynamic_slice(active_blocks, (device * RBD, 0), (RBD, 1)).reshape(-1)
    sent_points = call(
        spread_kernel, vmem_shape(N_COLS, PACKED, D, dtype=jnp.bfloat16), [SM, VM, VM]
    )(first_blocks, source_points, row_weights)
    points_here = exchange(sent_points, COLS)

    firsts = target_cluster.reshape(128, 128)[:, 0] - target_base
    target_means, target_logs = pl.pallas_call(
        target_means_kernel,
        out_shape=(vmem_shape(N_TGT, D), vmem_shape(1, N_TGT)),
        grid=(8,),
        in_specs=[
            SM,
            SM,
            pl.BlockSpec((2048, D), lambda k: (k, 0)),
            pl.BlockSpec((1, 1, 2048), lambda k: (k, 0, 0)),
        ],
        out_specs=(
            pl.BlockSpec((N_TGT, D), lambda k: (0, 0)),
            pl.BlockSpec((1, N_TGT), lambda k: (0, 0)),
        ),
        scratch_shapes=[pltpu.VMEM((N_TGT + PIECE, 2 * D), jnp.float32)],
        compiler_params=pltpu.CompilerParams(vmem_limit_bytes=24 << 20),
        cost_estimate=cost(1e9),
        name="target_means",
    )(target_base, firsts, in_hbm(target_points), in_hbm(target_cluster.reshape(8, 1, 2048)))

    group = lax.dynamic_slice_in_dim(active_blocks, row_index * N_COLS * RBD, N_COLS * RBD, 0)
    group_count = lax.dynamic_slice_in_dim(active_count, row_index * N_COLS * RBD, N_COLS * RBD)
    group_count = group_count.reshape(N_COLS, RBD)
    group = group.reshape(N_COLS, RBD, ACT)
    hit = group[:, :, 0] // CBD == col_index
    blocks = jnp.sum(jnp.where(hit[:, :, None], group % CBD, 0), axis=1).reshape(-1)
    counts = jnp.sum(jnp.where(hit, group_count, 0), axis=1)

    gains, source_logs, partial = call(
        coarse_start_kernel,
        (vmem_shape(N_SRC, N_TGT), vmem_shape(8, 128), vmem_shape(N_COLS, 8, 128)),
        [VM, VM],
        flops=1e9,
    )(in_vmem(gathered), in_vmem(target_means))
    gains, source_logs, target_logs = in_vmem(gains), in_vmem(source_logs), in_vmem(target_logs)

    def coarse_cols(parts, out_shape):
        return call(
            coarse_cols_kernel,
            out_shape,
            [VM] * (len(parts) + 2),
            [pltpu.VMEM((N_SRC, N_TGT), jnp.float32)],
        )(*[in_vmem(part) for part in parts], source_logs, gains)

    def coarse_rows(parts):
        return call(
            coarse_rows_kernel, vmem_shape(N_COLS, 8, 128), [VM] * (len(parts) + 2)
        )(*[in_vmem(part) for part in parts], target_logs, gains)

    for sweep in range(ITER_C):
        source_parts = [exchange(partial, COLS)]
        permuted = sweep in (0, ITER_C - 1)
        cols_shape = vmem_shape(1, N_TGT) if permuted else vmem_shape(N_ROWS, 1, N_TGT)
        cols_partial = coarse_cols(source_parts, cols_shape)
        if permuted:
            pair = lse_list([cols_partial, partner(cols_partial, "core", 1)])
            target_parts = four_along(pair, "x")
        else:
            target_parts = [exchange(cols_partial, ROWS)]
        if sweep + 1 < ITER_C:
            partial = coarse_rows(target_parts)

    slot_row = vmem_shape(N_COLS, 1, BLOCK)
    norms = pl.pallas_call(
        half_norms_kernel,
        out_shape=vmem_shape(CBD, 1, BLOCK),
        grid=(8,),
        in_specs=[pl.BlockSpec((2048, D), lambda k: (k, 0))],
        out_specs=pl.BlockSpec((8, 1, BLOCK), lambda k: (k, 0, 0)),
        compiler_params=pltpu.CompilerParams(vmem_limit_bytes=24 << 20),
        cost_estimate=cost(1e9),
        name="half_norms",
    )(in_hbm(target_points))
    fine_gains, halves, weights = call(
        products_kernel,
        (vmem_shape(N_COLS, BLOCK, WIDTH), slot_row, slot_row),
        [SM, SM, VM, ANY, ANY],
        [
            pltpu.VMEM((N_COLS, PACKED, D), jnp.bfloat16),
            pltpu.VMEM((N_COLS * ACT, BLOCK, D), jnp.bfloat16),
            pltpu.SemaphoreType.DMA((N_COLS, ACT + 1)),
        ],
        flops=1e9,
    )(counts, blocks, in_vmem(norms), in_hbm(points_here), in_hbm(target_points))
    fine_gains, halves, weights = in_vmem(fine_gains), in_vmem(halves), in_vmem(weights)
    column = vmem_shape(CBD, 1, BLOCK)
    values_scratch = pltpu.VMEM((CBD, 1, BLOCK), jnp.float32)
    work_scratch = pltpu.VMEM((BLOCK, WIDTH), jnp.float32)
    fine_shape = vmem_shape(N_COLS, BLOCK, WIDTH)
    best, fine_gains = call(
        first_pass_kernel,
        (column, fine_shape),
        [SM, SM, SM, SM, VM, VM, VM, VM, VM, VM],
        [values_scratch, pltpu.VMEM((N_TGT, 128), jnp.float32), work_scratch],
        input_output_aliases={9: 1},
    )(
        target_base,
        counts,
        blocks,
        firsts,
        *[in_vmem(part) for part in target_parts],
        target_cluster.reshape(CBD, 1, BLOCK),
        fine_gains,
    )
    best = lse_list([best, partner(best, "core", 1)])

    both, lam, fine_gains = call(
        second_pass_kernel,
        (vmem_shape(2 * CBD, 1, BLOCK), slot_row, fine_shape),
        [SM, SM, VM, VM, VM, VM, VM, VM],
        [values_scratch, work_scratch],
        input_output_aliases={7: 2},
    )(counts, blocks, *four_along_x(best), weights, in_vmem(fine_gains))
    other = partner(both, "core", 1)
    old, new = both[:CBD], other[:CBD]
    total = lse_list([old, new])
    mixed = both[CBD:] * jnp.exp2(old - total) + other[CBD:] * jnp.exp2(new - total)
    both = jnp.concatenate([total, mixed], axis=0)

    col_potential, col_adjoint, back = call(
        adjoint_kernel,
        (column, column, vmem_shape(N_COLS, 1, 2 * BLOCK)),
        [SM, SM, VM, VM, VM, VM, VM, VM, VM, VM, VM],
        [values_scratch],
    )(
        counts, blocks, *four_along_x(both), in_vmem(lam), halves, weights, col_weights,
        in_vmem(fine_gains),
    )
    back = exchange(back, COLS).reshape(N_COLS, 2 * BLOCK)
    chosen = (first_blocks // CBD)[:, None] == jnp.arange(N_COLS)[None, :]
    back = jnp.sum(jnp.where(chosen[:, :, None], back[None], 0.0), axis=1)
    return (
        back[:, :BLOCK].reshape(-1),
        col_potential.reshape(-1),
        back[:, BLOCK:].reshape(-1),
        col_adjoint.reshape(-1),
    )


def solution(mesh):
    split = Mesh(mesh.devices.reshape(4, 2, 4, 4), ALL)
    placed = (
        P(ALL, None),
        P(COLS, None),
        P(ALL),
        P(COLS),
        P(),
        P(),
        P(ALL),
        P(COLS),
    )
    return jax.shard_map(
        on_device,
        mesh=split,
        in_specs=placed,
        out_specs=(P(ALL), P(COLS), P(ALL), P(COLS)),
        check_vma=False,
    )
```

profile of v0, /device:TPU:1, one launch (start us, length us, event | category | flops | bytes accessed | tf_op | source)
XLA Modules:
  0.0 182.5 jit_solution(3161079897972177641)
XLA Ops:
  0.6 2.2 %shard_map.111 = f32[16,72,128]{2,1,0:T(8,128)} custom-call(s32[1]{0:T(128)} %bitcast.5.base, bf16[2048,128]{1,0:T(8,128)(2,1)} %points.7, s32[1,2048]{1,0:T(1,128)} %bitcast.53), custom_call_target="tpu_custom_call" | custom-call | flops 100000000 | bytes 4194304 | tf_op jit(solution)/shard_map/pallas_call | solution.py:499
  2.9 8.6 %all-to-all-start = ((f32[16,72,128]{2,1,0:T(8,128)}), f32[16,72,128]{2,1,0:T(8,128)S(1)}, u32[]{:S(2)}, u32[]{:S(2)}) async-start(f32[16,72,128]{2,1,0:T(8,128)} %shard_map.111), calls=%async_computation | async-start | bytes 1179648 | tf_op jit(solution)/shard_map/all_to_all | solution.py:464
  11.5 0.9 fusion.1.firsts.starts
  12.4 6.2 %target_means.1 = (f32[512,128]{1,0:T(8,128)S(1)}, f32[1,512]{1,0:T(1,128)S(1)}) custom-call(s32[1]{0:T(128)} %bitcast.3.base, s32[128]{0:T(128)S(1)} %fusion.1.firsts.starts, bf16[16384,128]{1,0:T(8,128)(2,1)} %y_hbm.1, s32[8,1,2048]{2,1,0:T(1,128)} %bitcast.48), custom_call_target="tpu_custom_call" | custom-call | flops 1000000000 | bytes 4194304 | tf_op jit(solution)/shard_map/target_means/pallas_call | solution.py:513
  18.6 3.8 %all-to-all-done.gathered = f32[16,72,128]{2,1,0:T(8,128)S(1)} async-done(((f32[16,72,128]{2,1,0:T(8,128)}), f32[16,72,128]{2,1,0:T(8,128)S(1)}, u32[]{:S(2)}, u32[]{:S(2)}) %all-to-all-start) | async-done | bytes 589856 | tf_op jit(solution)/shard_map/all_to_all | solution.py:464
  22.5 2.0 %shard_map.112 = (f32[1024,512]{1,0:T(8,128)S(1)}, f32[8,128]{1,0:T(8,128)S(1)}, f32[16,8,128]{2,1,0:T(8,128)S(1)}) custom-call(f32[16,72,128]{2,1,0:T(8,128)S(1)} %all-to-all-done.gathered, f32[512,128]{1,0:T(8,128)S(1)} %get-tuple-element.20.targets), custom_call_target="tpu_custom_call" | custom-call | flops 1000000000 | bytes 4194304 | tf_op jit(solution)/shard_map/pallas_call | solution.py:541
  24.5 9.9 %all_to_all.45.refs_0_ = f32[16,8,128]{2,1,0:T(8,128)S(1)} all-to-all(f32[16,8,128]{2,1,0:T(8,128)S(1)} %get-tuple-element.21), channel_id=1, replica_groups=mesh['x'=4,'core'=2,'y'=4,'z'=4] {'y','z'}, dimensions={0} | all-to-all | bytes 131072 | tf_op jit(solution)/shard_map/all_to_all | solution.py:464
  34.4 0.6 shard_map.113
  35.0 3.3 %collective-permute-start = (f32[1,512]{1,0:T(1,128)S(1)}, f32[1,512]{1,0:T(1,128)S(1)}, u32[]{:S(2)}, u32[]{:S(2)}) collective-permute-start(f32[1,512]{1,0:T(1,128)S(1)} %shard_map.113), channel_id=1, source_target_pairs={{0,16},{16,0},{1,17},{17,1},{2,18},{18,2},{3,19},{19,3},{4,20},{20... | collective-permute-start | bytes 6152 | tf_op jit(solution)/shard_map/ppermute | solution.py:469
  38.3 0.8 collective-permute-done
  39.1 1.3 collective-permute-start.1
  40.4 2.5 %collective-permute-start.2 = (f32[1,512]{1,0:T(1,128)S(1)}, f32[1,512]{1,0:T(1,128)S(1)}, u32[]{:S(2)}, u32[]{:S(2)}) collective-permute-start(f32[1,512]{1,0:T(1,128)S(1)} %multiply_add_fusion.3.refs_0_), channel_id=1, source_target_pairs={{0,64},{32,96},{64,0},{96,32},{1,65},{33,97},{65,1},{97,33},{2,66}... | collective-permute-start | bytes 6152 | tf_op jit(solution)/shard_map/ppermute | solution.py:469
  42.9 0.2 collective-permute-start.3
  43.1 1.3 collective-permute-done.2.refs_2_
  44.3 2.2 %collective-permute-done.3.refs_3_ = f32[1,512]{1,0:T(1,128)S(1)} collective-permute-done((f32[1,512]{1,0:T(1,128)S(1)}, f32[1,512]{1,0:T(1,128)S(1)}, u32[]{:S(2)}, u32[]{:S(2)}) %collective-permute-start.3) | collective-permute-done | bytes 2080 | tf_op jit(solution)/shard_map/ppermute | solution.py:469
  46.5 1.3 shard_map.114
  47.8 9.5 %all_to_all.46.refs_0_ = f32[16,8,128]{2,1,0:T(8,128)S(1)} all-to-all(f32[16,8,128]{2,1,0:T(8,128)S(1)} %shard_map.114), channel_id=1, replica_groups=mesh['x'=4,'core'=2,'y'=4,'z'=4] {'y','z'}, dimensions={0} | all-to-all | bytes 131072 | tf_op jit(solution)/shard_map/all_to_all | solution.py:464
  57.3 0.6 shard_map.115
  57.9 10.5 %all_to_all.47.refs_0_ = f32[8,1,512]{2,1,0:T(1,128)S(1)} all-to-all(f32[8,1,512]{2,1,0:T(1,128)S(1)} %shard_map.115), channel_id=1, replica_groups=mesh['x'=4,'core'=2,'y'=4,'z'=4] {'x','core'}, dimensions={0} | all-to-all | bytes 32768 | tf_op jit(solution)/shard_map/all_to_all | solution.py:464
  68.4 1.3 shard_map.116
  69.7 9.5 %all_to_all.48.refs_0_ = f32[16,8,128]{2,1,0:T(8,128)S(1)} all-to-all(f32[16,8,128]{2,1,0:T(8,128)S(1)} %shard_map.116), channel_id=1, replica_groups=mesh['x'=4,'core'=2,'y'=4,'z'=4] {'y','z'}, dimensions={0} | all-to-all | bytes 131072 | tf_op jit(solution)/shard_map/all_to_all | solution.py:464
  79.2 1.2 shard_map.117
  80.4 5.3 %all-to-all-start.5 = ((f32[8,1,512]{2,1,0:T(1,128)}), f32[8,1,512]{2,1,0:T(1,128)S(1)}, u32[]{:S(2)}, u32[]{:S(2)}) async-start(f32[8,1,512]{2,1,0:T(1,128)} %shard_map.117), calls=%async_computation.5 | async-start | bytes 32768 | tf_op jit(solution)/shard_map/all_to_all | solution.py:464
  85.7 4.7 %all-to-all-done.5.refs_0_ = f32[8,1,512]{2,1,0:T(1,128)S(1)} async-done(((f32[8,1,512]{2,1,0:T(1,128)}), f32[8,1,512]{2,1,0:T(1,128)S(1)}, u32[]{:S(2)}, u32[]{:S(2)}) %all-to-all-start.5) | async-done | bytes 16416 | tf_op jit(solution)/shard_map/all_to_all | solution.py:464
  90.4 2.0 %shard_map.118 = f32[16,8,128]{2,1,0:T(8,128)} custom-call(f32[8,1,512]{2,1,0:T(1,128)S(1)} %all-to-all-done.5.refs_0_, f32[1,512]{1,0:T(1,128)S(1)} %get-tuple-element.24.refs_4_.refs_1_, f32[1024,512]{1,0:T(8,128)S(1)} %get-tuple-element.23.refs_2_.refs_5_), custom_call_target="tpu_custom_call" | custom-call | flops 100000000 | bytes 4194304 | tf_op jit(solution)/shard_map/pallas_call | solution.py:558
  92.4 3.5 %all-to-all-start.6 = ((f32[16,8,128]{2,1,0:T(8,128)}), f32[16,8,128]{2,1,0:T(8,128)S(1)}, u32[]{:S(2)}, u32[]{:S(2)}) async-start(f32[16,8,128]{2,1,0:T(8,128)} %shard_map.118), calls=%async_computation.6 | async-start | bytes 131072 | tf_op jit(solution)/shard_map/all_to_all | solution.py:464
  95.9 0.8 fusion.17
  96.6 1.6 shard_map.120
  98.2 4.1 %all-to-all-done.6.refs_0_ = f32[16,8,128]{2,1,0:T(8,128)S(1)} async-done(((f32[16,8,128]{2,1,0:T(8,128)}), f32[16,8,128]{2,1,0:T(8,128)S(1)}, u32[]{:S(2)}, u32[]{:S(2)}) %all-to-all-start.6) | async-done | bytes 65568 | tf_op jit(solution)/shard_map/all_to_all | solution.py:464
  102.3 4.4 %all-to-all-start.7 = ((bf16[16,272,128]{2,1,0:T(8,128)(2,1)}), bf16[16,272,128]{2,1,0:T(8,128)(2,1)}, u32[]{:S(2)}, u32[]{:S(2)}) async-start(bf16[16,272,128]{2,1,0:T(8,128)(2,1)} %shard_map.120), calls=%async_computation.7 | async-start | bytes 2228224 | tf_op jit(solution)/shard_map/all_to_all | solution.py:464
  106.7 0.7 constant_dynamic-slice_fusion
  107.7 0.8 dynamic_slice.11
  108.8 0.6 shard_map.119
  109.4 1.9 %collective-permute-start.4 = (f32[1,512]{1,0:T(1,128)S(1)}, f32[1,512]{1,0:T(1,128)S(1)}, u32[]{:S(2)}, u32[]{:S(2)}) collective-permute-start(f32[1,512]{1,0:T(1,128)S(1)} %shard_map.119), channel_id=1, source_target_pairs={{0,16},{16,0},{1,17},{17,1},{2,18},{18,2},{3,19},{19,3},{4,20},{20... | collective-permute-start | bytes 6152 | tf_op jit(solution)/shard_map/ppermute | solution.py:469
  111.3 6.3 %half_norms.1.norms = f32[64,1,256]{2,1,0:T(1,128)S(1)} custom-call(bf16[16384,128]{1,0:T(8,128)(2,1)} %y_hbm.1), custom_call_target="tpu_custom_call" | custom-call | flops 1000000000 | bytes 4194304 | tf_op jit(solution)/shard_map/half_norms/pallas_call | solution.py:576
  117.8 0.4 collective-permute-start.5
  118.2 1.8 collective-permute-start.6
  119.9 1.8 collective-permute-start.7
  121.7 0.9 all-to-all-done.7.x_hbm
  122.7 4.9 %shard_map.121 = (f32[16,256,1024]{2,1,0:T(8,128)S(1)}, f32[16,1,256]{2,1,0:T(1,128)S(1)}, f32[16,1,256]{2,1,0:T(1,128)S(1)}) custom-call(s32[16]{0:T(128)S(1)} %select_reduce_fusion.1.counts, s32[64]{0:T(128)S(1)} %reshape.84.blocks, f32[64,1,256]{2,1,0:T(1,128)S(1)} %half_norms.1.norms, bf16[16,272,128]{2,1,0:T(8,128)(2,1)} %all-to-all-done.7.x_hbm, ...), custom_call_target="tpu_custom_call" | custom-call | flops 1000000000 | bytes 4194304 | tf_op jit(solution)/shard_map/pallas_call | solution.py:586
  127.6 6.9 %shard_map.122 = (f32[64,1,256]{2,1,0:T(1,128)S(1)}, f32[16,256,1024]{2,1,0:T(8,128)S(1)}) custom-call(s32[1]{0:T(128)} %bitcast.3.base, s32[16]{0:T(128)S(1)} %select_reduce_fusion.1.counts, s32[64]{0:T(128)S(1)} %reshape.84.blocks, s32[128]{0:T(128)S(1)} %fusion.1.firsts.starts, ...), custom_call_target="tpu_custom_call", output_to_operand_aliasing={{1}: (9, {})} | custom-call | flops 100000000 | bytes 4194304 | tf_op jit(solution)/shard_map/pallas_call | solution.py:602
  134.6 3.2 %collective-permute-start.8 = (f32[64,1,256]{2,1,0:T(1,128)S(1)}, f32[64,1,256]{2,1,0:T(1,128)S(1)}, u32[]{:S(2)}, u32[]{:S(2)}) collective-permute-start(f32[64,1,256]{2,1,0:T(1,128)S(1)} %get-tuple-element.26), channel_id=1, source_target_pairs={{0,16},{16,0},{1,17},{17,1},{2,18},{18,2},{3,19},{19,3},{4,20},{20... | collective-permute-start | bytes 196616 | tf_op jit(solution)/shard_map/ppermute | solution.py:469
  137.8 0.9 collective-permute-done.8
  138.7 0.3 multiply_add_fusion.1.l0
  138.9 0.9 collective-permute-start.10
  139.8 1.9 %collective-permute-start.11 = (f32[64,1,256]{2,1,0:T(1,128)S(1)}, f32[64,1,256]{2,1,0:T(1,128)S(1)}, u32[]{:S(2)}, u32[]{:S(2)}) collective-permute-start(f32[64,1,256]{2,1,0:T(1,128)S(1)} %multiply_add_fusion.1.l0), channel_id=1, source_target_pairs={{0,96},{32,64},{64,32},{96,0},{1,97},{33,65},{65,33},{97,1},{2,98}... | collective-permute-start | bytes 196616 | tf_op jit(solution)/shard_map/ppermute | solution.py:469
  141.7 1.9 %collective-permute-done.10.l2 = f32[64,1,256]{2,1,0:T(1,128)S(1)} collective-permute-done((f32[64,1,256]{2,1,0:T(1,128)S(1)}, f32[64,1,256]{2,1,0:T(1,128)S(1)}, u32[]{:S(2)}, u32[]{:S(2)}) %collective-permute-start.10) | collective-permute-done | bytes 65568 | tf_op jit(solution)/shard_map/ppermute | solution.py:469
  143.6 2.1 %collective-permute-done.11.l3 = f32[64,1,256]{2,1,0:T(1,128)S(1)} collective-permute-done((f32[64,1,256]{2,1,0:T(1,128)S(1)}, f32[64,1,256]{2,1,0:T(1,128)S(1)}, u32[]{:S(2)}, u32[]{:S(2)}) %collective-permute-start.11) | collective-permute-done | bytes 65568 | tf_op jit(solution)/shard_map/ppermute | solution.py:469
  145.8 6.5 %shard_map.123 = (f32[128,1,256]{2,1,0:T(1,128)S(1)}, f32[16,1,256]{2,1,0:T(1,128)S(1)}, f32[16,256,1024]{2,1,0:T(8,128)S(1)}) custom-call(s32[16]{0:T(128)S(1)} %select_reduce_fusion.1.counts, s32[64]{0:T(128)S(1)} %reshape.84.blocks, f32[64,1,256]{2,1,0:T(1,128)S(1)} %multiply_add_fusion.1.l0, ...), custom_call_target="tpu_custom_call", output_to_operand_aliasing={{2}: (7, {})} | custom-call | flops 100000000 | bytes 4194304 | tf_op jit(solution)/shard_map/pallas_call | solution.py:619
  152.3 1.2 collective-permute-start.12
  153.5 1.0 collective-permute-done.12
  154.5 0.4 fusion
  155.2 2.1 %collective-permute-start.14 = (f32[128,1,256]{2,1,0:T(1,128)S(1)}, f32[128,1,256]{2,1,0:T(1,128)S(1)}, u32[]{:S(2)}, u32[]{:S(2)}) collective-permute-start(f32[128,1,256]{2,1,0:T(1,128)S(1)} %pad_maximum_fusion.b0), channel_id=1, source_target_pairs={{0,64},{32,96},{64,0},{96,32},{1,65},{33,97},{65,1},{97,33},{2,66}... | collective-permute-start | bytes 393224 | tf_op jit(solution)/shard_map/ppermute | solution.py:469
  157.3 1.7 collective-permute-start.15
  159.0 0.8 collective-permute-done.13.b1
  159.8 3.5 %collective-permute-done.14.b2 = f32[128,1,256]{2,1,0:T(1,128)S(1)} collective-permute-done((f32[128,1,256]{2,1,0:T(1,128)S(1)}, f32[128,1,256]{2,1,0:T(1,128)S(1)}, u32[]{:S(2)}, u32[]{:S(2)}) %collective-permute-start.14) | collective-permute-done | bytes 131104 | tf_op jit(solution)/shard_map/ppermute | solution.py:469
  163.3 2.5 %collective-permute-done.15.b3 = f32[128,1,256]{2,1,0:T(1,128)S(1)} collective-permute-done((f32[128,1,256]{2,1,0:T(1,128)S(1)}, f32[128,1,256]{2,1,0:T(1,128)S(1)}, u32[]{:S(2)}, u32[]{:S(2)}) %collective-permute-start.15) | collective-permute-done | bytes 131104 | tf_op jit(solution)/shard_map/ppermute | solution.py:469
  165.9 5.3 %shard_map.124 = (f32[64,1,256]{2,1,0:T(1,128)S(1)}, f32[64,1,256]{2,1,0:T(1,128)S(1)}, f32[16,1,512]{2,1,0:T(1,128)}) custom-call(s32[16]{0:T(128)S(1)} %select_reduce_fusion.1.counts, s32[64]{0:T(128)S(1)} %reshape.84.blocks, f32[128,1,256]{2,1,0:T(1,128)S(1)} %pad_maximum_fusion.b0, f32[128,1,256]{2,1,0:T(1,128)S(1)} %collective-permute-done.13.b1, ...), custom_call_target="tpu_custom_call" | custom-call | flops 100000000 | bytes 4194304 | tf_op jit(solution)/shard_map/pallas_call | solution.py:632
  171.2 3.5 %all-to-all-start.8 = ((f32[16,1,512]{2,1,0:T(1,128)}), f32[16,1,512]{2,1,0:T(1,128)S(1)}, u32[]{:S(2)}, u32[]{:S(2)}) async-start(f32[16,1,512]{2,1,0:T(1,128)} %get-tuple-element.33), calls=%async_computation.8 | async-start | bytes 65536 | tf_op jit(solution)/shard_map/all_to_all | solution.py:464
  174.8 0.6 copy.45
  175.4 0.6 copy.46
  176.1 5.1 %all-to-all-done.8 = f32[16,1,512]{2,1,0:T(1,128)S(1)} async-done(((f32[16,1,512]{2,1,0:T(1,128)}), f32[16,1,512]{2,1,0:T(1,128)S(1)}, u32[]{:S(2)}, u32[]{:S(2)}) %all-to-all-start.8) | async-done | bytes 32800 | tf_op jit(solution)/shard_map/all_to_all | solution.py:464
  181.3 0.6 copy.39
  181.9 0.6 copy.40
  (34 shorter events, 1.3 us)
Async XLA Ops:
  2.9 19.6 %all-to-all-start = ((f32[16,72,128]{2,1,0:T(8,128)}), f32[16,72,128]{2,1,0:T(8,128)S(1)}, u32[]{:S(2)}, u32[]{:S(2)}) async-start(f32[16,72,128]{2,1,0:T(8,128)} %shard_map.111), calls=%async_computation | async-start | bytes 1179648 | tf_op jit(solution)/shard_map/all_to_all | solution.py:464
  35.0 4.1 %collective-permute-start = (f32[1,512]{1,0:T(1,128)S(1)}, f32[1,512]{1,0:T(1,128)S(1)}, u32[]{:S(2)}, u32[]{:S(2)}) collective-permute-start(f32[1,512]{1,0:T(1,128)S(1)} %shard_map.113), channel_id=1, source_target_pairs={{0,16},{16,0},{1,17},{17,1},{2,18},{18,2},{3,19},{19,3},{4,20},{20... | collective-permute-start | bytes 6152 | tf_op jit(solution)/shard_map/ppermute | solution.py:469
  39.1 3.9 %collective-permute-start.1 = (f32[1,512]{1,0:T(1,128)S(1)}, f32[1,512]{1,0:T(1,128)S(1)}, u32[]{:S(2)}, u32[]{:S(2)}) collective-permute-start(f32[1,512]{1,0:T(1,128)S(1)} %multiply_add_fusion.3.refs_0_), channel_id=1, source_target_pairs={{0,32},{32,0},{64,96},{96,64},{1,33},{33,1},{65,97},{97,65},{2,34}... | collective-permute-start | bytes 6152 | tf_op jit(solution)/shard_map/ppermute | solution.py:469
  40.4 3.9 %collective-permute-start.2 = (f32[1,512]{1,0:T(1,128)S(1)}, f32[1,512]{1,0:T(1,128)S(1)}, u32[]{:S(2)}, u32[]{:S(2)}) collective-permute-start(f32[1,512]{1,0:T(1,128)S(1)} %multiply_add_fusion.3.refs_0_), channel_id=1, source_target_pairs={{0,64},{32,96},{64,0},{96,32},{1,65},{33,97},{65,1},{97,33},{2,66}... | collective-permute-start | bytes 6152 | tf_op jit(solution)/shard_map/ppermute | solution.py:469
  42.9 3.6 %collective-permute-start.3 = (f32[1,512]{1,0:T(1,128)S(1)}, f32[1,512]{1,0:T(1,128)S(1)}, u32[]{:S(2)}, u32[]{:S(2)}) collective-permute-start(f32[1,512]{1,0:T(1,128)S(1)} %multiply_add_fusion.3.refs_0_), channel_id=1, source_target_pairs={{0,96},{32,64},{64,32},{96,0},{1,97},{33,65},{65,33},{97,1},{2,98}... | collective-permute-start | bytes 6152 | tf_op jit(solution)/shard_map/ppermute | solution.py:469
  57.3 39.4 %copy-start = (bf16[2048,128]{1,0:T(8,128)(2,1)S(1)}, bf16[2048,128]{1,0:T(8,128)(2,1)}, u32[]{:S(2)}) copy-start(bf16[2048,128]{1,0:T(8,128)(2,1)} %points.7) | copy-start | bytes 1572868
  57.3 39.4 %copy-start.3 = (f32[2048]{0:T(1024)S(1)}, f32[2048]{0:T(1024)}, u32[]{:S(2)}) copy-start(f32[2048]{0:T(1024)} %param.14) | copy-start | bytes 24580
  80.4 10.0 %all-to-all-start.5 = ((f32[8,1,512]{2,1,0:T(1,128)}), f32[8,1,512]{2,1,0:T(1,128)S(1)}, u32[]{:S(2)}, u32[]{:S(2)}) async-start(f32[8,1,512]{2,1,0:T(1,128)} %shard_map.117), calls=%async_computation.5 | async-start | bytes 32768 | tf_op jit(solution)/shard_map/all_to_all | solution.py:464
  92.4 10.0 %all-to-all-start.6 = ((f32[16,8,128]{2,1,0:T(8,128)}), f32[16,8,128]{2,1,0:T(8,128)S(1)}, u32[]{:S(2)}, u32[]{:S(2)}) async-start(f32[16,8,128]{2,1,0:T(8,128)} %shard_map.118), calls=%async_computation.6 | async-start | bytes 131072 | tf_op jit(solution)/shard_map/all_to_all | solution.py:464
  102.3 20.4 %all-to-all-start.7 = ((bf16[16,272,128]{2,1,0:T(8,128)(2,1)}), bf16[16,272,128]{2,1,0:T(8,128)(2,1)}, u32[]{:S(2)}, u32[]{:S(2)}) async-start(bf16[16,272,128]{2,1,0:T(8,128)(2,1)} %shard_map.120), calls=%async_computation.7 | async-start | bytes 2228224 | tf_op jit(solution)/shard_map/all_to_all | solution.py:464
  109.4 18.2 %copy-start.1 = (s32[16384]{0:T(1024)S(1)}, s32[16384]{0:T(1024)}, u32[]{:S(2)}) copy-start(s32[16384]{0:T(1024)} %param.11) | copy-start | bytes 196612
  109.4 8.4 %collective-permute-start.4 = (f32[1,512]{1,0:T(1,128)S(1)}, f32[1,512]{1,0:T(1,128)S(1)}, u32[]{:S(2)}, u32[]{:S(2)}) collective-permute-start(f32[1,512]{1,0:T(1,128)S(1)} %shard_map.119), channel_id=1, source_target_pairs={{0,16},{16,0},{1,17},{17,1},{2,18},{18,2},{3,19},{19,3},{4,20},{20... | collective-permute-start | bytes 6152 | tf_op jit(solution)/shard_map/ppermute | solution.py:469
  117.8 9.8 %collective-permute-start.5 = (f32[1,512]{1,0:T(1,128)S(1)}, f32[1,512]{1,0:T(1,128)S(1)}, u32[]{:S(2)}, u32[]{:S(2)}) collective-permute-start(f32[1,512]{1,0:T(1,128)S(1)} %multiply_add_fusion.2.p0), channel_id=1, source_target_pairs={{0,32},{32,0},{64,96},{96,64},{1,33},{33,1},{65,97},{97,65},{2,34}... | collective-permute-start | bytes 6152 | tf_op jit(solution)/shard_map/ppermute | solution.py:469
  118.2 9.4 %collective-permute-start.6 = (f32[1,512]{1,0:T(1,128)S(1)}, f32[1,512]{1,0:T(1,128)S(1)}, u32[]{:S(2)}, u32[]{:S(2)}) collective-permute-start(f32[1,512]{1,0:T(1,128)S(1)} %multiply_add_fusion.2.p0), channel_id=1, source_target_pairs={{0,64},{32,96},{64,0},{96,32},{1,65},{33,97},{65,1},{97,33},{2,66}... | collective-permute-start | bytes 6152 | tf_op jit(solution)/shard_map/ppermute | solution.py:469
  119.9 7.7 %collective-permute-start.7 = (f32[1,512]{1,0:T(1,128)S(1)}, f32[1,512]{1,0:T(1,128)S(1)}, u32[]{:S(2)}, u32[]{:S(2)}) collective-permute-start(f32[1,512]{1,0:T(1,128)S(1)} %multiply_add_fusion.2.p0), channel_id=1, source_target_pairs={{0,96},{32,64},{64,32},{96,0},{1,97},{33,65},{65,33},{97,1},{2,98}... | collective-permute-start | bytes 6152 | tf_op jit(solution)/shard_map/ppermute | solution.py:469
  134.6 4.1 %collective-permute-start.8 = (f32[64,1,256]{2,1,0:T(1,128)S(1)}, f32[64,1,256]{2,1,0:T(1,128)S(1)}, u32[]{:S(2)}, u32[]{:S(2)}) collective-permute-start(f32[64,1,256]{2,1,0:T(1,128)S(1)} %get-tuple-element.26), channel_id=1, source_target_pairs={{0,16},{16,0},{1,17},{17,1},{2,18},{18,2},{3,19},{19,3},{4,20},{20... | collective-permute-start | bytes 196616 | tf_op jit(solution)/shard_map/ppermute | solution.py:469
  138.9 4.7 %collective-permute-start.10 = (f32[64,1,256]{2,1,0:T(1,128)S(1)}, f32[64,1,256]{2,1,0:T(1,128)S(1)}, u32[]{:S(2)}, u32[]{:S(2)}) collective-permute-start(f32[64,1,256]{2,1,0:T(1,128)S(1)} %multiply_add_fusion.1.l0), channel_id=1, source_target_pairs={{0,64},{32,96},{64,0},{96,32},{1,65},{33,97},{65,1},{97,33},{2,66}... | collective-permute-start | bytes 196616 | tf_op jit(solution)/shard_map/ppermute | solution.py:469
  139.8 5.9 %collective-permute-start.11 = (f32[64,1,256]{2,1,0:T(1,128)S(1)}, f32[64,1,256]{2,1,0:T(1,128)S(1)}, u32[]{:S(2)}, u32[]{:S(2)}) collective-permute-start(f32[64,1,256]{2,1,0:T(1,128)S(1)} %multiply_add_fusion.1.l0), channel_id=1, source_target_pairs={{0,96},{32,64},{64,32},{96,0},{1,97},{33,65},{65,33},{97,1},{2,98}... | collective-permute-start | bytes 196616 | tf_op jit(solution)/shard_map/ppermute | solution.py:469
  141.7 4.1 %collective-permute-start.9 = (f32[64,1,256]{2,1,0:T(1,128)S(1)}, f32[64,1,256]{2,1,0:T(1,128)S(1)}, u32[]{:S(2)}, u32[]{:S(2)}) collective-permute-start(f32[64,1,256]{2,1,0:T(1,128)S(1)} %multiply_add_fusion.1.l0), channel_id=1, source_target_pairs={{0,32},{32,0},{64,96},{96,64},{1,33},{33,1},{65,97},{97,65},{2,34}... | collective-permute-start | bytes 196616 | tf_op jit(solution)/shard_map/ppermute | solution.py:469
  145.8 20.1 %copy-start.2 = (f32[16384]{0:T(1024)S(1)}, f32[16384]{0:T(1024)}, u32[]{:S(2)}) copy-start(f32[16384]{0:T(1024)} %param.15) | copy-start | bytes 196612
  152.3 2.2 %collective-permute-start.12 = (f32[128,1,256]{2,1,0:T(1,128)S(1)}, f32[128,1,256]{2,1,0:T(1,128)S(1)}, u32[]{:S(2)}, u32[]{:S(2)}) collective-permute-start(f32[128,1,256]{2,1,0:T(1,128)S(1)} %get-tuple-element.29), channel_id=1, source_target_pairs={{0,16},{16,0},{1,17},{17,1},{2,18},{18,2},{3,19},{19,3},{4,20},{20... | collective-permute-start | bytes 393224 | tf_op jit(solution)/shard_map/ppermute | solution.py:469
  155.1 4.8 %collective-permute-start.13 = (f32[128,1,256]{2,1,0:T(1,128)S(1)}, f32[128,1,256]{2,1,0:T(1,128)S(1)}, u32[]{:S(2)}, u32[]{:S(2)}) collective-permute-start(f32[128,1,256]{2,1,0:T(1,128)S(1)} %pad_maximum_fusion.b0), channel_id=1, source_target_pairs={{0,32},{32,0},{64,96},{96,64},{1,33},{33,1},{65,97},{97,65},{2,34}... | collective-permute-start | bytes 393224 | tf_op jit(solution)/shard_map/ppermute | solution.py:469
  155.2 8.2 %collective-permute-start.14 = (f32[128,1,256]{2,1,0:T(1,128)S(1)}, f32[128,1,256]{2,1,0:T(1,128)S(1)}, u32[]{:S(2)}, u32[]{:S(2)}) collective-permute-start(f32[128,1,256]{2,1,0:T(1,128)S(1)} %pad_maximum_fusion.b0), channel_id=1, source_target_pairs={{0,64},{32,96},{64,0},{96,32},{1,65},{33,97},{65,1},{97,33},{2,66}... | collective-permute-start | bytes 393224 | tf_op jit(solution)/shard_map/ppermute | solution.py:469
  157.3 8.6 %collective-permute-start.15 = (f32[128,1,256]{2,1,0:T(1,128)S(1)}, f32[128,1,256]{2,1,0:T(1,128)S(1)}, u32[]{:S(2)}, u32[]{:S(2)}) collective-permute-start(f32[128,1,256]{2,1,0:T(1,128)S(1)} %pad_maximum_fusion.b0), channel_id=1, source_target_pairs={{0,96},{32,64},{64,32},{96,0},{1,97},{33,65},{65,33},{97,1},{2,98}... | collective-permute-start | bytes 393224 | tf_op jit(solution)/shard_map/ppermute | solution.py:469
  171.2 9.9 %all-to-all-start.8 = ((f32[16,1,512]{2,1,0:T(1,128)}), f32[16,1,512]{2,1,0:T(1,128)S(1)}, u32[]{:S(2)}, u32[]{:S(2)}) async-start(f32[16,1,512]{2,1,0:T(1,128)} %get-tuple-element.33), calls=%async_computation.8 | async-start | bytes 65536 | tf_op jit(solution)/shard_map/all_to_all | solution.py:464
where the time goes:
time: 184 us; the launch traced here: 182 us
  Pallas kernels  49.6 us (27%)
  starting transfers between devices  49.5 us (27%)
  blocking collectives  39.3 us (21%)
  waiting for transfers between devices  35.7 us (19%)
  local copies, waits for them, and re-layouts  4.52 us (2%)
  other arithmetic  2.97 us (2%)
    all_to_all x4, blocking collectives, exchange(): return lax.all_to_all(x, axis, split_axis=0, concat_axis=0, tiled=True)  39.3 us
    all_to_all x5, starting transfers between devices, exchange(): return lax.all_to_all(x, axis, split_axis=0, concat_axis=0, tiled=True)  25.3 us
    ppermute x16, starting transfers between devices, partner(): return lax.ppermute(x, axis, [(k, k ^ step) for k in range(n)])  24.2 us
    all_to_all x5, waiting for transfers between devices, exchange(): return lax.all_to_all(x, axis, split_axis=0, concat_axis=0, tiled=True)  18.6 us
    ppermute x16, waiting for transfers between devices, partner(): return lax.ppermute(x, axis, [(k, k ^ step) for k in range(n)])  17.1 us
    pallas_call x1, Pallas kernels, on_device(): call(first_pass_kernel, (column, fine_shape), [SM, SM, SM, SM, VM, VM, VM...  6.93 us
    pallas_call x1, Pallas kernels, on_device(): call(second_pass_kernel, (vmem_shape(2 * CBD, 1, BLOCK), slot_row, fine_s...  6.54 us
    pallas_call x1, Pallas kernels, on_device(): pl.pallas_call(half_norms_kernel, out_shape=vmem_shape(CBD, 1, BLOCK), gr...  6.25 us
  transfers between devices with their start and end apart: 21, of which 15 were waited for; matrix products, arithmetic and copies ran while one was open for 3% of the time, Pallas kernels for 11%

commit v1 on v0

--- a/solution.py
+++ b/solution.py
@@ -22,8 +22,9 @@
 N_SRC = CL_DEV * N_COLS
 N_TGT = 512
 PTS_SRC = 2048
-WINDOW = 136
+PTS_TGT = 16384
 PIECE = 32
+TINY = 2.0**-80
 PACKED = BLOCK + 16
 
 SCALE = 2.8853900817779268
@@ -42,6 +43,10 @@
 
 def in_vmem(x):
     return pltpu.with_memory_space_constraint(x, pltpu.VMEM)
+
+
+def shape(*dims):
+    return pltpu.HBM(dims, jnp.float32)
 
 
 def in_hbm(x):
@@ -95,42 +100,69 @@
         out[peer, CL_DEV:, :] = tail
 
 
-def target_means_kernel(base, firsts, points, labels, means, logs, acc):
-    step = pl.program_id(0)
-
-    @pl.when(step == 0)
-    def _():
-        acc[...] = jnp.zeros_like(acc)
+def target_stats_kernel(base, firsts, labels, y_hbm, means, logs, norms, acc, ys, sems):
+    copies = [
+        pltpu.make_async_copy(
+            y_hbm.at[k * 2048 : (k + 1) * 2048, :], ys.at[k * 2048 : (k + 1) * 2048, :], sems.at[k]
+        )
+        for k in range(8)
+    ]
+    for copy in copies:
+        copy.start()
+    acc[...] = jnp.zeros_like(acc)
+    ones = jnp.full((8, 2 * D), 1.0, jnp.bfloat16)
 
     def piece(chunk, start, points_here):
-        at = slice(chunk * 256, (chunk + 1) * 256)
-        hits = one_hot(labels[0, :, at] - (start + base[0]), PIECE)
+        hits = one_hot(labels[chunk] - (start + base[0]), PIECE)
         window = pl.ds(pl.multiple_of(start, 8), PIECE)
         acc[window, :] += totals_and_counts(hits, points_here)
 
-    starts, extra = [], []
-    for chunk in range(8):
-        index = 2 * (step * 8 + chunk)
-        start = firsts[index] // 8 * 8
-        beyond = jnp.where(index + 2 < 128, firsts[jnp.minimum(index + 2, 127)], N_TGT - 1)
-        starts.append(start)
-        extra.append((beyond - start) // PIECE)
-        piece(chunk, start, points[chunk * 256 : (chunk + 1) * 256, :])
-    for chunk in range(8):
-        def more(k, carry, chunk=chunk):
-            piece(chunk, starts[chunk] + k * PIECE, points[chunk * 256 : (chunk + 1) * 256, :])
-            return carry
-
-        lax.fori_loop(1, extra[chunk] + 1, more, 0)
-
-    @pl.when(step == pl.num_programs(0) - 1)
-    def _():
-        mask = eye(128)
-        for part in range(4):
-            at = slice(part * 128, (part + 1) * 128)
-            counts = acc[at, D:]
-            means[at, :] = acc[at, :D] / counts
-            logs[:, at] = jnp.log2(to_row(counts, mask))
+    for step in range(8):
+        copies[step].wait()
+
+        def some(n, most, step=step):
+            for k in range(4):
+                chunk = step * 8 + n * 4 + k
+                points = ys[pl.ds(pl.multiple_of(chunk * BLOCK, BLOCK), BLOCK), :]
+                start = firsts[2 * chunk] // 8 * 8
+                piece(chunk, start, points)
+                beyond = firsts[jnp.minimum(2 * chunk + 2, 127)]
+                beyond = jnp.where(chunk < CBD - 1, beyond, N_TGT - 1)
+                most = jnp.maximum(most, (beyond - start) // PIECE)
+                wide = points.astype(jnp.float32)
+                square = wide * wide
+                high = square.astype(jnp.bfloat16)
+                low = (square - high.astype(jnp.float32)).astype(jnp.bfloat16)
+                both = jnp.concatenate([high, low], axis=1)
+                total = lax.dot_general(ones, both, NT, preferred_element_type=jnp.float32)
+                norms[chunk] = (0.5 * SCALE) * total[:1]
+            return most
+
+        most = lax.fori_loop(0, 2, some, 0)
+
+        @pl.when(most > 0)
+        def _(step=step):
+            def chunk_rest(chunk, carry):
+                start = firsts[2 * chunk] // 8 * 8
+                beyond = firsts[jnp.minimum(2 * chunk + 2, 127)]
+                beyond = jnp.where(chunk < CBD - 1, beyond, N_TGT - 1)
+
+                def more(k, carry):
+                    points = ys[pl.ds(pl.multiple_of(chunk * BLOCK, BLOCK), BLOCK), :]
+                    piece(chunk, start + k * PIECE, points)
+                    return carry
+
+                lax.fori_loop(1, (beyond - start) // PIECE + 1, more, 0)
+                return carry
+
+            lax.fori_loop(step * 8, step * 8 + 8, chunk_rest, 0)
+
+    mask = eye(128)
+    for part in range(4):
+        at = slice(part * 128, (part + 1) * 128)
+        counts = acc[at, D:]
+        means[at, :] = acc[at, :D] / counts
+        logs[:, at] = jnp.log2(to_row(counts, mask))
 
 
 def row_lse_chunk(scores):
@@ -173,9 +205,9 @@
     potential = target_logs[...] - lse_list(parts_of(gathered))
     for part in range(8):
         pieces = []
-        for piece in range(2):
-            at = part * 128 + piece * 64
-            pieces.append(row_lse_chunk(gains[at : at + 64, :] + potential))
+        for piece in range(1):
+            at = part * 128 + piece * 128
+            pieces.append(row_lse_chunk(gains[at : at + 128, :] + potential))
         out[0, part : part + 1, :] = to_row(jnp.concatenate(pieces, axis=0), mask)
     first = out[0]
     for peer in range(1, N_COLS):
@@ -230,18 +262,6 @@
     return copies
 
 
-def half_norms_kernel(points, out):
-    left = jnp.full((8, 2 * D), 1.0, jnp.bfloat16)
-    for b in range(8):
-        wide = points[b * BLOCK : (b + 1) * BLOCK, :].astype(jnp.float32)
-        square = wide * wide
-        high = square.astype(jnp.bfloat16)
-        low = (square - high.astype(jnp.float32)).astype(jnp.bfloat16)
-        right = jnp.concatenate([high, low], axis=1)
-        total = lax.dot_general(left, right, NT, preferred_element_type=jnp.float32)
-        out[b] = (0.5 * SCALE) * total[:1]
-
-
 def products_kernel(counts, blocks, norms, x_hbm, y_hbm, gains, halves, weights, xs, ys, sems):
     copies = start_copies(counts, blocks, x_hbm, y_hbm, xs, ys, sems)
     mask = eye(128)
@@ -274,9 +294,94 @@
     return jnp.concatenate(rows, axis=1)
 
 
-CHUNK = 16
+CHUNK = 8
 CHUNKS = BLOCK // CHUNK
 WIDTH = ACT * BLOCK
+
+
+def merge_columns(slot, counts, blocks, values, best, mixed, result, mean):
+    for a in range(ACT):
+        block = blocks[slot * ACT + a]
+        at = slice(a * BLOCK, (a + 1) * BLOCK)
+        here = jnp.where(a < counts[slot], result[:, at] - values[block], lowest)
+        old = best[block]
+        top = jnp.maximum(old, here)
+        old_part, new_part = jnp.exp2(old - top), jnp.exp2(here - top)
+        both = old_part + new_part
+        best[block] = top + jnp.log2(both)
+        if mean is not None:
+            part = jnp.where(a < counts[slot], mean[:, at], 0.0)
+            mixed[block] = (mixed[block] * old_part + part * new_part) / both
+
+
+GROUP = 256
+FAST = 8
+
+
+def fast_slot(slot, counts, blocks, gains, values, best, least, sums, cols, weights=None, mixed=None, lam_out=None):
+    potential = slot_potential(slot, counts, blocks, values)
+    mask = eye(128)
+    if weights is not None:
+        w_row = weights[slot]
+        for h in range(2):
+            at = slice(h * 128, (h + 1) * 128)
+            cols[at, 0:1] = to_column(w_row[:, at], mask)
+    sums[...] = jnp.zeros(sums.shape, jnp.float32)
+
+    def group(step, carry):
+        total = sums[:8, :]
+        weighted = sums[8:, :]
+        for k in range(GROUP // FAST):
+            at = pl.ds(pl.multiple_of(step * GROUP + k * FAST, FAST), FAST)
+            scores = gains[slot, at, :] + potential
+            highest = jnp.max(scores, axis=1, keepdims=True)
+            entries = jnp.exp2(scores - highest)
+            mass = jnp.sum(entries, axis=1, keepdims=True)
+            if lam_out is not None:
+                cols[at, 1:2] = highest + jnp.log2(mass)
+            scale = 1.0 / mass
+            part = (entries * scale).reshape(FAST // 8, 8, WIDTH)
+            total = total + jnp.sum(part, axis=0)
+            if weights is not None:
+                part = (entries * (scale * cols[at, 0:1])).reshape(FAST // 8, 8, WIDTH)
+                weighted = weighted + jnp.sum(part, axis=0)
+        sums[:8, :] = total
+        if weights is not None:
+            sums[8:, :] = weighted
+        return carry
+
+    lax.fori_loop(0, BLOCK // GROUP, group, 0)
+    total = jnp.sum(sums[:8, :], axis=0, keepdims=True)
+    mean = None if weights is None else jnp.sum(sums[8:, :], axis=0, keepdims=True) / total
+    for a in range(ACT):
+        part = jnp.where(a < counts[slot], total[:, a * BLOCK : (a + 1) * BLOCK], 1.0)
+        least[...] = jnp.minimum(least[...], part)
+    merge_columns(slot, counts, blocks, values, best, mixed, jnp.log2(total), mean)
+    if lam_out is not None:
+        for h in range(2):
+            at = slice(h * 128, (h + 1) * 128)
+            lam_out[slot, :, at] = to_row(cols[at, 1:2], mask)
+
+
+def fine_pass(counts, blocks, gains, work, values, best, least, sums, cols, weights=None, mixed=None, lam_out=None):
+    clear(best, mixed)
+    least[...] = jnp.ones(least.shape, jnp.float32)
+    each_slot(
+        counts,
+        lambda slot: fast_slot(
+            slot, counts, blocks, gains, values, best, least, sums, cols, weights, mixed, lam_out
+        ),
+    )
+
+    @pl.when(jnp.logical_not(jnp.min(least[...]) > TINY))
+    def _():
+        clear(best, mixed)
+        each_slot(
+            counts,
+            lambda slot: fine_slot(
+                slot, counts, blocks, gains, work, values, best, weights, mixed, lam_out
+            ),
+        )
 
 
 def fine_slot(slot, counts, blocks, gains, work, values, best, weights=None, mixed=None, lam_out=None):
@@ -308,23 +413,12 @@
             weighted = weighted + jnp.sum(value.reshape(CHUNK // 8, 8, WIDTH), axis=0)
     total = jnp.sum(total, axis=0, keepdims=True)
     result = highest + jnp.log2(total)
-    if weights is not None:
-        mean = jnp.sum(weighted, axis=0, keepdims=True) / total
-    for a in range(ACT):
-        block = blocks[slot * ACT + a]
-        at = slice(a * BLOCK, (a + 1) * BLOCK)
-        here = jnp.where(a < counts[slot], result[:, at] - values[block], lowest)
-        old = best[block]
-        top = jnp.maximum(old, here)
-        old_part, new_part = jnp.exp2(old - top), jnp.exp2(here - top)
-        both = old_part + new_part
-        best[block] = top + jnp.log2(both)
-        if weights is not None:
-            mixed[block] = (mixed[block] * old_part + mean[:, at] * new_part) / both
+    mean = None if weights is None else jnp.sum(weighted, axis=0, keepdims=True) / total
+    merge_columns(slot, counts, blocks, values, best, mixed, result, mean)
     if lam_out is not None:
         for h in range(2):
             at = slice(h * 128, (h + 1) * 128)
-            lam_out[slot, :, at] = to_row(jnp.concatenate(lams[h * 8 : (h + 1) * 8], axis=0), mask)
+            lam_out[slot, :, at] = to_row(jnp.concatenate(lams[h * CHUNKS // 2 : (h + 1) * CHUNKS // 2], axis=0), mask)
 
 
 def clear(best, mixed=None):
@@ -348,58 +442,37 @@
 
 
 def first_pass_kernel(
-    base, counts, blocks, starts, p0, p1, p2, p3, labels, gains, best, kept, values, table, work
+    base, counts, blocks, p0, p1, p2, p3, labels, gains, best, kept, values, work, least, sums, cols
 ):
-    clear(best)
-    mask = eye(128)
     cluster_values = -lse_list([p0[...], p1[...], p2[...], p3[...]])
+    index = labels[...] - base[0]
+    found = jnp.zeros((128, 128), jnp.float32)
     for part in range(4):
-        at = slice(part * 128, (part + 1) * 128)
-        table[at, :] = jnp.broadcast_to(to_column(cluster_values[:, at], mask), (128, 128))
-
-    def spread(step, carry):
-        for n in range(8):
-            block, h = step * 4 + n // 2, n % 2
-            first = starts[2 * block + h] // 8 * 8
-            first = pl.multiple_of(jnp.minimum(first, N_TGT - WINDOW), 8)
-            at = slice(h * 128, (h + 1) * 128)
-            index = lax.broadcasted_iota(jnp.int32, (WINDOW, 128), 0)
-            hit = index == labels[block, :, at] - (base[0] + first)
-            window = table[pl.ds(first, WINDOW), :]
-            values[block, :, at] = jnp.sum(jnp.where(hit, window, 0.0), axis=0, keepdims=True)
-        return carry
-
-    lax.fori_loop(0, CBD // 4, spread, 0)
-    each_slot(
-        counts, lambda slot: fine_slot(slot, counts, blocks, gains, work, values, best)
-    )
+        row = cluster_values[:, part * 128 : (part + 1) * 128]
+        picked = jnp.take_along_axis(
+            jnp.broadcast_to(row, (128, 128)), index & 127, axis=1, mode="promise_in_bounds"
+        )
+        found = jnp.where(index >> 7 == part, picked, found)
+    for chunk in range(128):
+        at = slice(chunk % 2 * 128, (chunk % 2 + 1) * 128)
+        values[chunk // 2, :, at] = found[chunk : chunk + 1, :]
+    fine_pass(counts, blocks, gains, work, values, best, least, sums, cols)
 
 
 def second_pass_kernel(
-    counts, blocks, l0, l1, l2, l3, weights, gains, both, lam, kept, values, work
+    counts, blocks, l0, l1, l2, l3, weights, gains, best, mixed, lam, kept, values, work, least, sums, cols
 ):
-    best, mixed = both.at[:CBD], both.at[CBD:]
-    clear(best, mixed)
     values[...] = -lse_list([l0[...], l1[...], l2[...], l3[...]])
-    each_slot(
-        counts,
-        lambda slot: fine_slot(
-            slot, counts, blocks, gains, work, values, best, weights, mixed, lam
-        ),
-    )
+    fine_pass(counts, blocks, gains, work, values, best, least, sums, cols, weights, mixed, lam)
 
 
 def adjoint_kernel(
-    counts, blocks, b0, b1, b2, b3, lam, halves, weights, col_weights, gains,
-    potential_out, adjoint_out, back, values,
+    counts, blocks, l0, l1, l2, l3, lam, halves, weights, col_weights, gains,
+    potential_out, back, values,
 ):
-    parts = [b0, b1, b2, b3]
-    total = lse_list([part[:CBD] for part in parts])
-    mixed = [part[CBD:] * jnp.exp2(part[:CBD] - total) for part in parts]
-    mixed = (mixed[0] + mixed[1]) + (mixed[2] + mixed[3])
+    total = lse_list([l0[...], l1[...], l2[...], l3[...]])
     values[...] = -total
     potential_out[...] = total * (-1.0 / SCALE)
-    adjoint_out[...] = mixed + col_weights[...]
     back[...] = jnp.zeros(back.shape, jnp.float32)
     mask = eye(128)
 
@@ -428,9 +501,49 @@
     each_slot(counts, body)
 
 
+def plan_kernel(row, col, lists_hbm, counts_hbm, counts, blocks, owners, lists, found, sems):
+    first = pl.multiple_of(row[0] * 128, 128)
+    copies = [
+        pltpu.make_async_copy(lists_hbm.at[:, pl.ds(first, 128)], lists, sems.at[0]),
+        pltpu.make_async_copy(counts_hbm.at[row[0]], found, sems.at[1]),
+    ]
+    for copy in copies:
+        copy.start()
+    for copy in copies:
+        copy.wait()
+    for q in range(RBD):
+        owners[q] = lists[0, col[0] * RBD + q] >> 6
+
+    def fill(slot, carry):
+        count = jnp.int32(0)
+        chosen = [jnp.int32(0)] * ACT
+        for q in range(RBD):
+            index = slot * RBD + q
+            here = (lists[0, index] >> 6) == col[0]
+            count = jnp.where(here, found[index], count)
+            chosen = [
+                jnp.where(here, lists[a, index] & (CBD - 1), old) for a, old in enumerate(chosen)
+            ]
+        counts[slot] = count
+        for a in range(ACT):
+            blocks[slot * ACT + a] = chosen[a]
+        return carry
+
+    lax.fori_loop(0, N_COLS, fill, 0)
+
+
+def home_kernel(owners, back, potential, adjoint):
+    for q in range(RBD):
+        got = back[owners[q]]
+        for h in range(2):
+            at = slice(2 * q + h, 2 * q + h + 1)
+            potential[at, :] = got[:, h * 128 : (h + 1) * 128]
+            adjoint[at, :] = got[:, BLOCK + h * 128 : BLOCK + (h + 1) * 128]
+
+
 def spread_kernel(owners, points, weights, out):
     for q in range(RBD):
-        owner = owners[q] // CBD
+        owner = owners[q]
         out[owner, :BLOCK, :] = points[q * BLOCK : (q + 1) * BLOCK, :]
         rest = weights[q]
         pieces = []
@@ -503,40 +616,40 @@
 
     row_weights = row_weight.reshape(RBD, 2, 128)
     col_weights = col_weight.reshape(CBD, 1, BLOCK)
-    first_blocks = lax.dynamic_slice(active_blocks, (device * RBD, 0), (RBD, 1)).reshape(-1)
+    counts, blocks, owners = pl.pallas_call(
+        plan_kernel,
+        out_shape=tuple(jax.ShapeDtypeStruct((n,), jnp.int32) for n in (N_COLS, N_COLS * ACT, RBD)),
+        in_specs=[SM, SM, ANY, ANY],
+        out_specs=(SM, SM, SM),
+        scratch_shapes=[
+            pltpu.SMEM((ACT, 128), jnp.int32),
+            pltpu.SMEM((128,), jnp.int32),
+            pltpu.SemaphoreType.DMA((2,)),
+        ],
+        name="plan",
+    )(
+        row_index.reshape(1).astype(jnp.int32),
+        col_index.reshape(1).astype(jnp.int32),
+        in_hbm(active_blocks.T),
+        in_hbm(active_count.reshape(8, 128)),
+    )
     sent_points = call(
         spread_kernel, vmem_shape(N_COLS, PACKED, D, dtype=jnp.bfloat16), [SM, VM, VM]
-    )(first_blocks, source_points, row_weights)
+    )(owners, in_hbm(source_points), in_hbm(row_weights))
     points_here = exchange(sent_points, COLS)
 
     firsts = target_cluster.reshape(128, 128)[:, 0] - target_base
-    target_means, target_logs = pl.pallas_call(
-        target_means_kernel,
-        out_shape=(vmem_shape(N_TGT, D), vmem_shape(1, N_TGT)),
-        grid=(8,),
-        in_specs=[
-            SM,
-            SM,
-            pl.BlockSpec((2048, D), lambda k: (k, 0)),
-            pl.BlockSpec((1, 1, 2048), lambda k: (k, 0, 0)),
+    target_means, target_logs, norms = call(
+        target_stats_kernel,
+        (vmem_shape(N_TGT, D), vmem_shape(1, N_TGT), vmem_shape(CBD, 1, BLOCK)),
+        [SM, SM, VM, ANY],
+        [
+            pltpu.VMEM((N_TGT + PIECE, 2 * D), jnp.float32),
+            pltpu.VMEM((PTS_TGT, D), jnp.bfloat16),
+            pltpu.SemaphoreType.DMA((8,)),
         ],
-        out_specs=(
-            pl.BlockSpec((N_TGT, D), lambda k: (0, 0)),
-            pl.BlockSpec((1, N_TGT), lambda k: (0, 0)),
-        ),
-        scratch_shapes=[pltpu.VMEM((N_TGT + PIECE, 2 * D), jnp.float32)],
-        compiler_params=pltpu.CompilerParams(vmem_limit_bytes=24 << 20),
-        cost_estimate=cost(1e9),
-        name="target_means",
-    )(target_base, firsts, in_hbm(target_points), in_hbm(target_cluster.reshape(8, 1, 2048)))
-
-    group = lax.dynamic_slice_in_dim(active_blocks, row_index * N_COLS * RBD, N_COLS * RBD, 0)
-    group_count = lax.dynamic_slice_in_dim(active_count, row_index * N_COLS * RBD, N_COLS * RBD)
-    group_count = group_count.reshape(N_COLS, RBD)
-    group = group.reshape(N_COLS, RBD, ACT)
-    hit = group[:, :, 0] // CBD == col_index
-    blocks = jnp.sum(jnp.where(hit[:, :, None], group % CBD, 0), axis=1).reshape(-1)
-    counts = jnp.sum(jnp.where(hit, group_count, 0), axis=1)
+        flops=1e9,
+    )(target_base, firsts, target_cluster.reshape(CBD, 1, BLOCK), in_hbm(target_points))
 
     gains, source_logs, partial = call(
         coarse_start_kernel,
@@ -573,16 +686,6 @@
             partial = coarse_rows(target_parts)
 
     slot_row = vmem_shape(N_COLS, 1, BLOCK)
-    norms = pl.pallas_call(
-        half_norms_kernel,
-        out_shape=vmem_shape(CBD, 1, BLOCK),
-        grid=(8,),
-        in_specs=[pl.BlockSpec((2048, D), lambda k: (k, 0))],
-        out_specs=pl.BlockSpec((8, 1, BLOCK), lambda k: (k, 0, 0)),
-        compiler_params=pltpu.CompilerParams(vmem_limit_bytes=24 << 20),
-        cost_estimate=cost(1e9),
-        name="half_norms",
-    )(in_hbm(target_points))
     fine_gains, halves, weights = call(
         products_kernel,
         (vmem_shape(N_COLS, BLOCK, WIDTH), slot_row, slot_row),
@@ -598,53 +701,62 @@
     column = vmem_shape(CBD, 1, BLOCK)
     values_scratch = pltpu.VMEM((CBD, 1, BLOCK), jnp.float32)
     work_scratch = pltpu.VMEM((BLOCK, WIDTH), jnp.float32)
+    fast_scratch = [
+        pltpu.VMEM((1, BLOCK), jnp.float32),
+        pltpu.VMEM((16, WIDTH), jnp.float32),
+        pltpu.VMEM((BLOCK, 8), jnp.float32),
+    ]
     fine_shape = vmem_shape(N_COLS, BLOCK, WIDTH)
     best, fine_gains = call(
         first_pass_kernel,
         (column, fine_shape),
-        [SM, SM, SM, SM, VM, VM, VM, VM, VM, VM],
-        [values_scratch, pltpu.VMEM((N_TGT, 128), jnp.float32), work_scratch],
-        input_output_aliases={9: 1},
+        [SM, SM, SM, VM, VM, VM, VM, VM, VM],
+        [values_scratch, work_scratch, *fast_scratch],
+        input_output_aliases={8: 1},
     )(
         target_base,
         counts,
         blocks,
-        firsts,
         *[in_vmem(part) for part in target_parts],
-        target_cluster.reshape(CBD, 1, BLOCK),
+        target_cluster.reshape(128, 128),
         fine_gains,
     )
     best = lse_list([best, partner(best, "core", 1)])
 
-    both, lam, fine_gains = call(
+    best, mixed, lam, fine_gains = call(
         second_pass_kernel,
-        (vmem_shape(2 * CBD, 1, BLOCK), slot_row, fine_shape),
+        (column, column, slot_row, fine_shape),
         [SM, SM, VM, VM, VM, VM, VM, VM],
-        [values_scratch, work_scratch],
-        input_output_aliases={7: 2},
+        [values_scratch, work_scratch, *fast_scratch],
+        input_output_aliases={7: 3},
     )(counts, blocks, *four_along_x(best), weights, in_vmem(fine_gains))
-    other = partner(both, "core", 1)
-    old, new = both[:CBD], other[:CBD]
-    total = lse_list([old, new])
-    mixed = both[CBD:] * jnp.exp2(old - total) + other[CBD:] * jnp.exp2(new - total)
-    both = jnp.concatenate([total, mixed], axis=0)
-
-    col_potential, col_adjoint, back = call(
+    other = partner(best, "core", 1)
+    other_mixed = partner(mixed, "core", 1)
+    total = lse_list([best, other])
+    mixed = mixed * jnp.exp2(best - total) + other_mixed * jnp.exp2(other - total)
+    best_parts = four_along(total, "x")
+    mixed_parts = four_along(mixed, "x")
+
+    col_potential, back = call(
         adjoint_kernel,
-        (column, column, vmem_shape(N_COLS, 1, 2 * BLOCK)),
+        (shape(CBD, 1, BLOCK), vmem_shape(N_COLS, 1, 2 * BLOCK)),
         [SM, SM, VM, VM, VM, VM, VM, VM, VM, VM, VM],
         [values_scratch],
     )(
-        counts, blocks, *four_along_x(both), in_vmem(lam), halves, weights, col_weights,
-        in_vmem(fine_gains),
-    )
-    back = exchange(back, COLS).reshape(N_COLS, 2 * BLOCK)
-    chosen = (first_blocks // CBD)[:, None] == jnp.arange(N_COLS)[None, :]
-    back = jnp.sum(jnp.where(chosen[:, :, None], back[None], 0.0), axis=1)
+        counts, blocks, *[in_vmem(part) for part in best_parts], in_vmem(lam), halves,
+        weights, col_weights, in_vmem(fine_gains),
+    )
+    total = lse_list(best_parts)
+    mixed = [m * jnp.exp2(part - total) for m, part in zip(mixed_parts, best_parts)]
+    col_adjoint = ((mixed[0] + mixed[1]) + (mixed[2] + mixed[3])) + col_weights
+    back = exchange(back, COLS)
+    row_potential, row_adjoint = call(
+        home_kernel, (shape(16, 128), shape(16, 128)), [SM, VM]
+    )(owners, in_vmem(back))
     return (
-        back[:, :BLOCK].reshape(-1),
+        row_potential.reshape(-1),
         col_potential.reshape(-1),
-        back[:, BLOCK:].reshape(-1),
+        row_adjoint.reshape(-1),
         col_adjoint.reshape(-1),
     )
 

time: 184 us -> 176 us (0.957)
  blocking collectives: 39.3 us -> 50.2 us
  waiting for transfers between devices: 35.7 us -> 27.8 us
  Pallas kernels: 49.6 us -> 43.2 us
  local copies, waits for them, and re-layouts: 4.52 us -> 1.52 us
  starting transfers between devices: 49.5 us -> 46.7 us
    all_to_all x4 -> x5, blocking collectives: 39.3 us -> 50.2 us  [exchange(): return lax.all_to_all(x, axis, split_axis=0, concat_axis=0, tiled=True)]
    ppermute x16 -> x20, waiting for transfers between devices: 17.1 us -> 9.85 us  [partner(): return lax.ppermute(x, axis, [(k, k ^ step) for k in range(n)])]
    all_to_all x5 -> x4, starting transfers between devices: 25.3 us -> 20.9 us  [exchange(): return lax.all_to_all(x, axis, split_axis=0, concat_axis=0, tiled=True)]
    pallas_call x5 -> x6, Pallas kernels: 31.3 us -> 27.1 us  [the longest x1 7.34 us: on_device(): call(target_stats_kernel, (vmem_shape(N_TGT, D), vmem_shape(1, N_TGT), vm...]
    pallas_call x3, Pallas kernels: 4.59 us -> 2.5 us  [coarse_rows(): call(coarse_rows_kernel, vmem_shape(N_COLS, 8, 128), [VM] * (len(parts) +...]
    ppermute x16 -> x20, starting transfers between devices: 24.2 us -> 25.8 us  [partner(): return lax.ppermute(x, axis, [(k, k ^ step) for k in range(n)])]
    all_to_all x5 -> x4, waiting for transfers between devices: 18.6 us -> 18 us  [exchange(): return lax.all_to_all(x, axis, split_axis=0, concat_axis=0, tiled=True)]
  transfers between devices with their start and end apart: 21 -> 24, of which waited for: 15 -> 14; matrix products, arithmetic and copies ran while one was open for 3% -> 1% of each run, Pallas kernels for 11% -> 13%
where the time goes in v1:
time: 176 us; the launch traced here: 173 us
  blocking collectives  50.2 us (29%)
  starting transfers between devices  46.7 us (27%)
  Pallas kernels  43.2 us (25%)
  waiting for transfers between devices  27.8 us (16%)
  other arithmetic  3.19 us (2%)
    all_to_all x5, blocking collectives, exchange(): return lax.all_to_all(x, axis, split_axis=0, concat_axis=0, tiled=True)  50.2 us
    ppermute x20, starting transfers between devices, partner(): return lax.ppermute(x, axis, [(k, k ^ step) for k in range(n)])  25.8 us
    all_to_all x4, starting transfers between devices, exchange(): return lax.all_to_all(x, axis, split_axis=0, concat_axis=0, tiled=True)  20.9 us
    all_to_all x4, waiting for transfers between devices, exchange(): return lax.all_to_all(x, axis, split_axis=0, concat_axis=0, tiled=True)  18 us
    ppermute x20, waiting for transfers between devices, partner(): return lax.ppermute(x, axis, [(k, k ^ step) for k in range(n)])  9.85 us
    pallas_call x1, Pallas kernels, on_device(): call(target_stats_kernel, (vmem_shape(N_TGT, D), vmem_shape(1, N_TGT), vm...  7.34 us
    pallas_call x1, Pallas kernels, on_device(): call(second_pass_kernel, (column, column, slot_row, fine_shape), [SM, SM,...  6.62 us
    pallas_call x1, Pallas kernels, on_device(): call(adjoint_kernel, (shape(CBD, 1, BLOCK), vmem_shape(N_COLS, 1, 2 * BLO...  5.17 us
  transfers between devices with their start and end apart: 24, of which 14 were waited for; matrix products, arithmetic and copies ran while one was open for 1% of the time, Pallas kernels for 13%

profile of v1, /device:TPU:1, one launch (start us, length us, event | category | flops | bytes accessed | tf_op | source)
XLA Modules:
  0.0 173.4 jit_solution(7450178825544458949)
XLA Ops:
  0.6 2.2 %shard_map.111 = f32[16,72,128]{2,1,0:T(8,128)} custom-call(s32[1]{0:T(128)} %bitcast.5.base, bf16[2048,128]{1,0:T(8,128)(2,1)} %points.3, s32[1,2048]{1,0:T(1,128)} %bitcast.22), custom_call_target="tpu_custom_call" | custom-call | flops 100000000 | bytes 4194304 | tf_op jit(solution)/shard_map/pallas_call | solution.py:612
  2.8 8.6 %all-to-all-start = ((f32[16,72,128]{2,1,0:T(8,128)}), f32[16,72,128]{2,1,0:T(8,128)S(1)}, u32[]{:S(2)}, u32[]{:S(2)}) async-start(f32[16,72,128]{2,1,0:T(8,128)} %shard_map.111), calls=%async_computation | async-start | bytes 1179648 | tf_op jit(solution)/shard_map/all_to_all | solution.py:577
  11.4 0.9 fusion.firsts
  12.4 0.8 copy-done
  13.2 7.3 %shard_map.112 = (f32[512,128]{1,0:T(8,128)S(1)}, f32[1,512]{1,0:T(1,128)S(1)}, f32[64,1,256]{2,1,0:T(1,128)S(1)}) custom-call(s32[1]{0:T(128)} %bitcast.4.base, s32[128]{0:T(128)S(1)} %fusion.firsts, s32[64,1,256]{2,1,0:T(1,128)S(1)} %bitcast.16, bf16[16384,128]{1,0:T(8,128)(2,1)} %y_hbm.3), custom_call_target="tpu_custom_call" | custom-call | flops 1000000000 | bytes 4194304 | tf_op jit(solution)/shard_map/pallas_call | solution.py:642
  20.6 1.8 %all-to-all-done.gathered = f32[16,72,128]{2,1,0:T(8,128)S(1)} async-done(((f32[16,72,128]{2,1,0:T(8,128)}), f32[16,72,128]{2,1,0:T(8,128)S(1)}, u32[]{:S(2)}, u32[]{:S(2)}) %all-to-all-start) | async-done | bytes 589856 | tf_op jit(solution)/shard_map/all_to_all | solution.py:577
  22.4 2.0 %shard_map.113 = (f32[1024,512]{1,0:T(8,128)S(1)}, f32[8,128]{1,0:T(8,128)S(1)}, f32[16,8,128]{2,1,0:T(8,128)S(1)}) custom-call(f32[16,72,128]{2,1,0:T(8,128)S(1)} %all-to-all-done.gathered, f32[512,128]{1,0:T(8,128)S(1)} %get-tuple-element.29.targets), custom_call_target="tpu_custom_call" | custom-call | flops 1000000000 | bytes 4194304 | tf_op jit(solution)/shard_map/pallas_call | solution.py:654
  24.4 11.1 %all_to_all.45.refs_0_ = f32[16,8,128]{2,1,0:T(8,128)S(1)} all-to-all(f32[16,8,128]{2,1,0:T(8,128)S(1)} %get-tuple-element.30), channel_id=1, replica_groups=mesh['x'=4,'core'=2,'y'=4,'z'=4] {'y','z'}, dimensions={0} | all-to-all | bytes 131072 | tf_op jit(solution)/shard_map/all_to_all | solution.py:577
  35.6 0.6 shard_map.114
  36.2 2.7 %collective-permute-start = (f32[1,512]{1,0:T(1,128)S(1)}, f32[1,512]{1,0:T(1,128)S(1)}, u32[]{:S(2)}, u32[]{:S(2)}) collective-permute-start(f32[1,512]{1,0:T(1,128)S(1)} %shard_map.114), channel_id=1, source_target_pairs={{0,16},{16,0},{1,17},{17,1},{2,18},{18,2},{3,19},{19,3},{4,20},{20... | collective-permute-start | bytes 6152 | tf_op jit(solution)/shard_map/ppermute | solution.py:582
  38.9 0.8 collective-permute-done
  39.8 2.6 %collective-permute-start.3 = (f32[1,512]{1,0:T(1,128)S(1)}, f32[1,512]{1,0:T(1,128)S(1)}, u32[]{:S(2)}, u32[]{:S(2)}) collective-permute-start(f32[1,512]{1,0:T(1,128)S(1)} %multiply_add_fusion.4.refs_0_), channel_id=1, source_target_pairs={{0,96},{32,64},{64,32},{96,0},{1,97},{33,65},{65,33},{97,1},{2,98}... | collective-permute-start | bytes 6152 | tf_op jit(solution)/shard_map/ppermute | solution.py:582
  42.3 0.5 collective-permute-start.2
  42.8 0.3 collective-permute-start.1
  43.1 0.4 collective-permute-done.3.refs_3_
  43.5 2.8 %collective-permute-done.2.refs_2_ = f32[1,512]{1,0:T(1,128)S(1)} collective-permute-done((f32[1,512]{1,0:T(1,128)S(1)}, f32[1,512]{1,0:T(1,128)S(1)}, u32[]{:S(2)}, u32[]{:S(2)}) %collective-permute-start.2) | collective-permute-done | bytes 2080 | tf_op jit(solution)/shard_map/ppermute | solution.py:582
  46.3 0.6 shard_map.115
  46.9 9.5 %all_to_all.46.refs_0_ = f32[16,8,128]{2,1,0:T(8,128)S(1)} all-to-all(f32[16,8,128]{2,1,0:T(8,128)S(1)} %shard_map.115), channel_id=1, replica_groups=mesh['x'=4,'core'=2,'y'=4,'z'=4] {'y','z'}, dimensions={0} | all-to-all | bytes 131072 | tf_op jit(solution)/shard_map/all_to_all | solution.py:577
  56.4 0.6 shard_map.116
  57.0 10.9 %all_to_all.47.refs_0_ = f32[8,1,512]{2,1,0:T(1,128)S(1)} all-to-all(f32[8,1,512]{2,1,0:T(1,128)S(1)} %shard_map.116), channel_id=1, replica_groups=mesh['x'=4,'core'=2,'y'=4,'z'=4] {'x','core'}, dimensions={0} | all-to-all | bytes 32768 | tf_op jit(solution)/shard_map/all_to_all | solution.py:577
  67.9 0.6 shard_map.117
  68.5 9.5 %all_to_all.48.refs_0_ = f32[16,8,128]{2,1,0:T(8,128)S(1)} all-to-all(f32[16,8,128]{2,1,0:T(8,128)S(1)} %shard_map.117), channel_id=1, replica_groups=mesh['x'=4,'core'=2,'y'=4,'z'=4] {'y','z'}, dimensions={0} | all-to-all | bytes 131072 | tf_op jit(solution)/shard_map/all_to_all | solution.py:577
  78.0 0.6 shard_map.118
  78.6 9.1 %all_to_all.49.refs_0_ = f32[8,1,512]{2,1,0:T(1,128)S(1)} all-to-all(f32[8,1,512]{2,1,0:T(1,128)S(1)} %shard_map.118), channel_id=1, replica_groups=mesh['x'=4,'core'=2,'y'=4,'z'=4] {'x','core'}, dimensions={0} | all-to-all | bytes 32768 | tf_op jit(solution)/shard_map/all_to_all | solution.py:577
  87.7 1.3 shard_map.119
  89.0 3.5 %all-to-all-start.6 = ((f32[16,8,128]{2,1,0:T(8,128)}), f32[16,8,128]{2,1,0:T(8,128)S(1)}, u32[]{:S(2)}, u32[]{:S(2)}) async-start(f32[16,8,128]{2,1,0:T(8,128)} %shard_map.119), calls=%async_computation.6 | async-start | bytes 131072 | tf_op jit(solution)/shard_map/all_to_all | solution.py:577
  92.5 2.3 %plan.1 = (s32[16]{0:T(128)}, s32[64]{0:T(128)}, s32[8]{0:T(128)}) custom-call(s32[1]{0:T(128)} %bitcast.row, s32[1]{0:T(128)} %bitcast.1.col, s32[4,1024]{1,0:T(4,128)} %bitcast.21, s32[8,128]{1,0:T(8,128)} %bitcast.24), custom_call_target="tpu_custom_call" | custom-call | tf_op jit(solution)/shard_map/plan/pallas_call | solution.py:619
  94.8 0.7 copy-done.5
  95.5 2.1 %shard_map.121 = bf16[16,272,128]{2,1,0:T(8,128)(2,1)} custom-call(s32[8]{0:T(128)S(1)} %copy-done.5, bf16[2048,128]{1,0:T(8,128)(2,1)} %points.3, f32[8,2,128]{2,1,0:T(2,128)} %bitcast.23), custom_call_target="tpu_custom_call" | custom-call | flops 100000000 | bytes 4194304 | tf_op jit(solution)/shard_map/pallas_call | solution.py:636
  97.6 1.3 all-to-all-done.6.refs_0_
  98.9 5.3 %all-to-all-start.7 = ((bf16[16,272,128]{2,1,0:T(8,128)(2,1)}), bf16[16,272,128]{2,1,0:T(8,128)(2,1)}, u32[]{:S(2)}, u32[]{:S(2)}) async-start(bf16[16,272,128]{2,1,0:T(8,128)(2,1)} %shard_map.121), calls=%async_computation.7 | async-start | bytes 2228224 | tf_op jit(solution)/shard_map/all_to_all | solution.py:577
  104.3 0.6 shard_map.120
  104.9 1.5 collective-permute-start.4
  106.4 0.8 collective-permute-done.4
  107.2 1.0 collective-permute-start.7
  108.2 1.2 collective-permute-start.6
  109.4 1.2 collective-permute-start.5
  110.6 9.9 %all-to-all-done.7.x_hbm = bf16[16,272,128]{2,1,0:T(8,128)(2,1)} async-done(((bf16[16,272,128]{2,1,0:T(8,128)(2,1)}), bf16[16,272,128]{2,1,0:T(8,128)(2,1)}, u32[]{:S(2)}, u32[]{:S(2)}) %all-to-all-start.7) | async-done | bytes 1114144 | tf_op jit(solution)/shard_map/all_to_all | solution.py:577
  120.5 4.9 %shard_map.122 = (f32[16,256,1024]{2,1,0:T(8,128)S(1)}, f32[16,1,256]{2,1,0:T(1,128)S(1)}, f32[16,1,256]{2,1,0:T(1,128)S(1)}) custom-call(s32[16]{0:T(128)S(1)} %copy-done.3, s32[64]{0:T(128)S(1)} %copy-done.4, f32[64,1,256]{2,1,0:T(1,128)S(1)} %get-tuple-element.34.norms, bf16[16,272,128]{2,1,0:T(8,128)(2,1)} %all-to-all-done.7.x_hbm, bf16[16384,128]{1,0:T(8,128)(2,1)} %y_hbm.3), custom_call_target="tpu_custom_call" | custom-call | flops 1000000000 | bytes 4194304 | tf_op jit(solution)/shard_map/pallas_call | solution.py:689
  125.5 4.5 %shard_map.123 = (f32[64,1,256]{2,1,0:T(1,128)S(1)}, f32[16,256,1024]{2,1,0:T(8,128)S(1)}) custom-call(s32[1]{0:T(128)} %bitcast.4.base, s32[16]{0:T(128)S(1)} %copy-done.3, s32[64]{0:T(128)S(1)} %copy-done.4, f32[1,512]{1,0:T(1,128)S(1)} %multiply_add_fusion.3.p0, f32[1,512]{1,0:T(1,128)S(1)} %collective-permute-done.5.p1, ...), custom_call_target="tpu_custom_call", output_to_operand_aliasing={{1}: (8, {})} | custom-call | flops 100000000 | bytes 4194304 | tf_op jit(solution)/shard_map/pallas_call | solution.py:710
  129.9 3.3 %collective-permute-start.8 = (f32[64,1,256]{2,1,0:T(1,128)S(1)}, f32[64,1,256]{2,1,0:T(1,128)S(1)}, u32[]{:S(2)}, u32[]{:S(2)}) collective-permute-start(f32[64,1,256]{2,1,0:T(1,128)S(1)} %get-tuple-element.36), channel_id=1, source_target_pairs={{0,16},{16,0},{1,17},{17,1},{2,18},{18,2},{3,19},{19,3},{4,20},{20... | collective-permute-start | bytes 196616 | tf_op jit(solution)/shard_map/ppermute | solution.py:582
  133.2 0.9 collective-permute-done.8
  134.4 1.0 collective-permute-start.11
  135.3 1.2 collective-permute-start.10
  136.6 1.1 collective-permute-start.9
  137.7 1.1 collective-permute-done.11.l3
  138.8 1.3 collective-permute-done.10.l2
  140.1 0.6 collective-permute-done.9.l1
  140.6 6.6 %shard_map.124 = (f32[64,1,256]{2,1,0:T(1,128)S(1)}, f32[64,1,256]{2,1,0:T(1,128)S(1)}, f32[16,1,256]{2,1,0:T(1,128)S(1)}, f32[16,256,1024]{2,1,0:T(8,128)S(1)}) custom-call(s32[16]{0:T(128)S(1)} %copy-done.3, s32[64]{0:T(128)S(1)} %copy-done.4, f32[64,1,256]{2,1,0:T(1,128)S(1)} %multiply_add_fusion.2.l0, ...), custom_call_target="tpu_custom_call", output_to_operand_aliasing={{3}: (7, {})} | custom-call | flops 100000000 | bytes 4194304 | tf_op jit(solution)/shard_map/pallas_call | solution.py:726
  147.3 1.6 collective-permute-start.12
  148.9 0.8 collective-permute-done.12
  149.7 0.4 collective-permute-done.16
  150.1 0.4 multiply_add_fusion
  150.5 1.8 %collective-permute-start.15 = (f32[64,1,256]{2,1,0:T(1,128)S(1)}, f32[64,1,256]{2,1,0:T(1,128)S(1)}, u32[]{:S(2)}, u32[]{:S(2)}) collective-permute-start(f32[64,1,256]{2,1,0:T(1,128)S(1)} %get-tuple-element.49.l0), channel_id=1, source_target_pairs={{0,96},{32,64},{64,32},{96,0},{1,97},{33,65},{65,33},{97,1},{2,98}... | collective-permute-start | bytes 196616 | tf_op jit(solution)/shard_map/ppermute | solution.py:582
  152.3 0.8 collective-permute-start.14
  153.2 0.7 collective-permute-start.13
  153.9 1.7 collective-permute-start.19
  155.6 0.8 collective-permute-start.18
  156.4 0.7 collective-permute-start.17
  157.1 5.2 %shard_map.125 = (f32[64,1,256]{2,1,0:T(1,128)}, f32[16,1,512]{2,1,0:T(1,128)}) custom-call(s32[16]{0:T(128)S(1)} %copy-done.3, s32[64]{0:T(128)S(1)} %copy-done.4, f32[64,1,256]{2,1,0:T(1,128)S(1)} %get-tuple-element.49.l0, f32[64,1,256]{2,1,0:T(1,128)S(1)} %collective-permute-done.13.l1, f32[64,1,256]{2,1,0:T(1,128)S(1)} %collective-permute-done.14.l2, ...), custom_call_target="tpu_custom_call" | custom-call | flops 100000000 | bytes 4194304 | tf_op jit(solution)/shard_map/pallas_call | solution.py:740
  162.3 3.5 %all-to-all-start.8 = ((f32[16,1,512]{2,1,0:T(1,128)}), f32[16,1,512]{2,1,0:T(1,128)S(1)}, u32[]{:S(2)}, u32[]{:S(2)}) async-start(f32[16,1,512]{2,1,0:T(1,128)} %get-tuple-element.43), calls=%async_computation.8 | async-start | bytes 65536 | tf_op jit(solution)/shard_map/all_to_all | solution.py:577
  165.8 1.5 add_add_fusion
  167.3 4.9 %all-to-all-done.8.back = f32[16,1,512]{2,1,0:T(1,128)S(1)} async-done(((f32[16,1,512]{2,1,0:T(1,128)}), f32[16,1,512]{2,1,0:T(1,128)S(1)}, u32[]{:S(2)}, u32[]{:S(2)}) %all-to-all-start.8) | async-done | bytes 32800 | tf_op jit(solution)/shard_map/all_to_all | solution.py:577
  172.2 1.2 shard_map.126
  (26 shorter events, 0.4 us)
Async XLA Ops:
  2.8 19.6 %all-to-all-start = ((f32[16,72,128]{2,1,0:T(8,128)}), f32[16,72,128]{2,1,0:T(8,128)S(1)}, u32[]{:S(2)}, u32[]{:S(2)}) async-start(f32[16,72,128]{2,1,0:T(8,128)} %shard_map.111), calls=%async_computation | async-start | bytes 1179648 | tf_op jit(solution)/shard_map/all_to_all | solution.py:577
  12.4 0.8 copy-start
  36.2 3.6 %collective-permute-start = (f32[1,512]{1,0:T(1,128)S(1)}, f32[1,512]{1,0:T(1,128)S(1)}, u32[]{:S(2)}, u32[]{:S(2)}) collective-permute-start(f32[1,512]{1,0:T(1,128)S(1)} %shard_map.114), channel_id=1, source_target_pairs={{0,16},{16,0},{1,17},{17,1},{2,18},{18,2},{3,19},{19,3},{4,20},{20... | collective-permute-start | bytes 6152 | tf_op jit(solution)/shard_map/ppermute | solution.py:582
  39.8 3.7 %collective-permute-start.3 = (f32[1,512]{1,0:T(1,128)S(1)}, f32[1,512]{1,0:T(1,128)S(1)}, u32[]{:S(2)}, u32[]{:S(2)}) collective-permute-start(f32[1,512]{1,0:T(1,128)S(1)} %multiply_add_fusion.4.refs_0_), channel_id=1, source_target_pairs={{0,96},{32,64},{64,32},{96,0},{1,97},{33,65},{65,33},{97,1},{2,98}... | collective-permute-start | bytes 6152 | tf_op jit(solution)/shard_map/ppermute | solution.py:582
  42.3 3.9 %collective-permute-start.2 = (f32[1,512]{1,0:T(1,128)S(1)}, f32[1,512]{1,0:T(1,128)S(1)}, u32[]{:S(2)}, u32[]{:S(2)}) collective-permute-start(f32[1,512]{1,0:T(1,128)S(1)} %multiply_add_fusion.4.refs_0_), channel_id=1, source_target_pairs={{0,64},{32,96},{64,0},{96,32},{1,65},{33,97},{65,1},{97,33},{2,66}... | collective-permute-start | bytes 6152 | tf_op jit(solution)/shard_map/ppermute | solution.py:582
  42.8 3.4 %collective-permute-start.1 = (f32[1,512]{1,0:T(1,128)S(1)}, f32[1,512]{1,0:T(1,128)S(1)}, u32[]{:S(2)}, u32[]{:S(2)}) collective-permute-start(f32[1,512]{1,0:T(1,128)S(1)} %multiply_add_fusion.4.refs_0_), channel_id=1, source_target_pairs={{0,32},{32,0},{64,96},{96,64},{1,33},{33,1},{65,97},{97,65},{2,34}... | collective-permute-start | bytes 6152 | tf_op jit(solution)/shard_map/ppermute | solution.py:582
  89.0 10.0 %all-to-all-start.6 = ((f32[16,8,128]{2,1,0:T(8,128)}), f32[16,8,128]{2,1,0:T(8,128)S(1)}, u32[]{:S(2)}, u32[]{:S(2)}) async-start(f32[16,8,128]{2,1,0:T(8,128)} %shard_map.119), calls=%async_computation.6 | async-start | bytes 131072 | tf_op jit(solution)/shard_map/all_to_all | solution.py:577
  94.8 25.7 %copy-start.3 = (s32[16]{0:T(128)S(1)}, s32[16]{0:T(128)}, u32[]{:S(2)}) copy-start(s32[16]{0:T(128)} %get-tuple-element.27.counts) | copy-start | bytes 196
  94.8 25.7 %copy-start.4 = (s32[64]{0:T(128)S(1)}, s32[64]{0:T(128)}, u32[]{:S(2)}) copy-start(s32[64]{0:T(128)} %get-tuple-element.28.blocks) | copy-start | bytes 772
  94.8 0.7 copy-start.5
  98.9 21.6 %all-to-all-start.7 = ((bf16[16,272,128]{2,1,0:T(8,128)(2,1)}), bf16[16,272,128]{2,1,0:T(8,128)(2,1)}, u32[]{:S(2)}, u32[]{:S(2)}) async-start(bf16[16,272,128]{2,1,0:T(8,128)(2,1)} %shard_map.121), calls=%async_computation.7 | async-start | bytes 2228224 | tf_op jit(solution)/shard_map/all_to_all | solution.py:577
  104.3 21.2 %copy-start.1 = (s32[16384]{0:T(1024)S(1)}, s32[16384]{0:T(1024)}, u32[]{:S(2)}) copy-start(s32[16384]{0:T(1024)} %param.11) | copy-start | bytes 196612
  104.9 2.4 %collective-permute-start.4 = (f32[1,512]{1,0:T(1,128)S(1)}, f32[1,512]{1,0:T(1,128)S(1)}, u32[]{:S(2)}, u32[]{:S(2)}) collective-permute-start(f32[1,512]{1,0:T(1,128)S(1)} %shard_map.120), channel_id=1, source_target_pairs={{0,16},{16,0},{1,17},{17,1},{2,18},{18,2},{3,19},{19,3},{4,20},{20... | collective-permute-start | bytes 6152 | tf_op jit(solution)/shard_map/ppermute | solution.py:582
  107.2 18.2 %collective-permute-start.7 = (f32[1,512]{1,0:T(1,128)S(1)}, f32[1,512]{1,0:T(1,128)S(1)}, u32[]{:S(2)}, u32[]{:S(2)}) collective-permute-start(f32[1,512]{1,0:T(1,128)S(1)} %multiply_add_fusion.3.p0), channel_id=1, source_target_pairs={{0,96},{32,64},{64,32},{96,0},{1,97},{33,65},{65,33},{97,1},{2,98}... | collective-permute-start | bytes 6152 | tf_op jit(solution)/shard_map/ppermute | solution.py:582
  108.2 17.2 %collective-permute-start.6 = (f32[1,512]{1,0:T(1,128)S(1)}, f32[1,512]{1,0:T(1,128)S(1)}, u32[]{:S(2)}, u32[]{:S(2)}) collective-permute-start(f32[1,512]{1,0:T(1,128)S(1)} %multiply_add_fusion.3.p0), channel_id=1, source_target_pairs={{0,64},{32,96},{64,0},{96,32},{1,65},{33,97},{65,1},{97,33},{2,66}... | collective-permute-start | bytes 6152 | tf_op jit(solution)/shard_map/ppermute | solution.py:582
  109.4 16.0 %collective-permute-start.5 = (f32[1,512]{1,0:T(1,128)S(1)}, f32[1,512]{1,0:T(1,128)S(1)}, u32[]{:S(2)}, u32[]{:S(2)}) collective-permute-start(f32[1,512]{1,0:T(1,128)S(1)} %multiply_add_fusion.3.p0), channel_id=1, source_target_pairs={{0,32},{32,0},{64,96},{96,64},{1,33},{33,1},{65,97},{97,65},{2,34}... | collective-permute-start | bytes 6152 | tf_op jit(solution)/shard_map/ppermute | solution.py:582
  129.9 4.2 %collective-permute-start.8 = (f32[64,1,256]{2,1,0:T(1,128)S(1)}, f32[64,1,256]{2,1,0:T(1,128)S(1)}, u32[]{:S(2)}, u32[]{:S(2)}) collective-permute-start(f32[64,1,256]{2,1,0:T(1,128)S(1)} %get-tuple-element.36), channel_id=1, source_target_pairs={{0,16},{16,0},{1,17},{17,1},{2,18},{18,2},{3,19},{19,3},{4,20},{20... | collective-permute-start | bytes 196616 | tf_op jit(solution)/shard_map/ppermute | solution.py:582
  134.4 4.4 %collective-permute-start.11 = (f32[64,1,256]{2,1,0:T(1,128)S(1)}, f32[64,1,256]{2,1,0:T(1,128)S(1)}, u32[]{:S(2)}, u32[]{:S(2)}) collective-permute-start(f32[64,1,256]{2,1,0:T(1,128)S(1)} %multiply_add_fusion.2.l0), channel_id=1, source_target_pairs={{0,96},{32,64},{64,32},{96,0},{1,97},{33,65},{65,33},{97,1},{2,98}... | collective-permute-start | bytes 196616 | tf_op jit(solution)/shard_map/ppermute | solution.py:582
  135.3 4.7 %collective-permute-start.10 = (f32[64,1,256]{2,1,0:T(1,128)S(1)}, f32[64,1,256]{2,1,0:T(1,128)S(1)}, u32[]{:S(2)}, u32[]{:S(2)}) collective-permute-start(f32[64,1,256]{2,1,0:T(1,128)S(1)} %multiply_add_fusion.2.l0), channel_id=1, source_target_pairs={{0,64},{32,96},{64,0},{96,32},{1,65},{33,97},{65,1},{97,33},{2,66}... | collective-permute-start | bytes 196616 | tf_op jit(solution)/shard_map/ppermute | solution.py:582
  136.6 4.1 %collective-permute-start.9 = (f32[64,1,256]{2,1,0:T(1,128)S(1)}, f32[64,1,256]{2,1,0:T(1,128)S(1)}, u32[]{:S(2)}, u32[]{:S(2)}) collective-permute-start(f32[64,1,256]{2,1,0:T(1,128)S(1)} %multiply_add_fusion.2.l0), channel_id=1, source_target_pairs={{0,32},{32,0},{64,96},{96,64},{1,33},{33,1},{65,97},{97,65},{2,34}... | collective-permute-start | bytes 196616 | tf_op jit(solution)/shard_map/ppermute | solution.py:582
  140.6 16.5 %copy-start.2 = (f32[16384]{0:T(1024)S(1)}, f32[16384]{0:T(1024)}, u32[]{:S(2)}) copy-start(f32[16384]{0:T(1024)} %param.15) | copy-start | bytes 196612
  147.3 2.5 %collective-permute-start.12 = (f32[64,1,256]{2,1,0:T(1,128)S(1)}, f32[64,1,256]{2,1,0:T(1,128)S(1)}, u32[]{:S(2)}, u32[]{:S(2)}) collective-permute-start(f32[64,1,256]{2,1,0:T(1,128)S(1)} %get-tuple-element.39), channel_id=1, source_target_pairs={{0,16},{16,0},{1,17},{17,1},{2,18},{18,2},{3,19},{19,3},{4,20},{20... | collective-permute-start | bytes 196616 | tf_op jit(solution)/shard_map/ppermute | solution.py:582
  148.8 1.3 collective-permute-start.16
  150.5 5.9 %collective-permute-start.15 = (f32[64,1,256]{2,1,0:T(1,128)S(1)}, f32[64,1,256]{2,1,0:T(1,128)S(1)}, u32[]{:S(2)}, u32[]{:S(2)}) collective-permute-start(f32[64,1,256]{2,1,0:T(1,128)S(1)} %get-tuple-element.49.l0), channel_id=1, source_target_pairs={{0,96},{32,64},{64,32},{96,0},{1,97},{33,65},{65,33},{97,1},{2,98}... | collective-permute-start | bytes 196616 | tf_op jit(solution)/shard_map/ppermute | solution.py:582
  152.3 4.8 %collective-permute-start.14 = (f32[64,1,256]{2,1,0:T(1,128)S(1)}, f32[64,1,256]{2,1,0:T(1,128)S(1)}, u32[]{:S(2)}, u32[]{:S(2)}) collective-permute-start(f32[64,1,256]{2,1,0:T(1,128)S(1)} %get-tuple-element.49.l0), channel_id=1, source_target_pairs={{0,64},{32,96},{64,0},{96,32},{1,65},{33,97},{65,1},{97,33},{2,66}... | collective-permute-start | bytes 196616 | tf_op jit(solution)/shard_map/ppermute | solution.py:582
  153.2 4.0 %collective-permute-start.13 = (f32[64,1,256]{2,1,0:T(1,128)S(1)}, f32[64,1,256]{2,1,0:T(1,128)S(1)}, u32[]{:S(2)}, u32[]{:S(2)}) collective-permute-start(f32[64,1,256]{2,1,0:T(1,128)S(1)} %get-tuple-element.49.l0), channel_id=1, source_target_pairs={{0,32},{32,0},{64,96},{96,64},{1,33},{33,1},{65,97},{97,65},{2,34}... | collective-permute-start | bytes 196616 | tf_op jit(solution)/shard_map/ppermute | solution.py:582
  153.9 11.9 %collective-permute-start.19 = (f32[64,1,256]{2,1,0:T(1,128)S(1)}, f32[64,1,256]{2,1,0:T(1,128)S(1)}, u32[]{:S(2)}, u32[]{:S(2)}) collective-permute-start(f32[64,1,256]{2,1,0:T(1,128)S(1)} %get-tuple-element.48), channel_id=1, source_target_pairs={{0,96},{32,64},{64,32},{96,0},{1,97},{33,65},{65,33},{97,1},{2,98}... | collective-permute-start | bytes 196616 | tf_op jit(solution)/shard_map/ppermute | solution.py:582
  155.6 10.2 %collective-permute-start.18 = (f32[64,1,256]{2,1,0:T(1,128)S(1)}, f32[64,1,256]{2,1,0:T(1,128)S(1)}, u32[]{:S(2)}, u32[]{:S(2)}) collective-permute-start(f32[64,1,256]{2,1,0:T(1,128)S(1)} %get-tuple-element.48), channel_id=1, source_target_pairs={{0,64},{32,96},{64,0},{96,32},{1,65},{33,97},{65,1},{97,33},{2,66}... | collective-permute-start | bytes 196616 | tf_op jit(solution)/shard_map/ppermute | solution.py:582
  156.4 9.4 %collective-permute-start.17 = (f32[64,1,256]{2,1,0:T(1,128)S(1)}, f32[64,1,256]{2,1,0:T(1,128)S(1)}, u32[]{:S(2)}, u32[]{:S(2)}) collective-permute-start(f32[64,1,256]{2,1,0:T(1,128)S(1)} %get-tuple-element.48), channel_id=1, source_target_pairs={{0,32},{32,0},{64,96},{96,64},{1,33},{33,1},{65,97},{97,65},{2,34}... | collective-permute-start | bytes 196616 | tf_op jit(solution)/shard_map/ppermute | solution.py:582
  157.1 15.1 %copy-start.6 = (s32[8]{0:T(128)S(1)}, s32[8]{0:T(128)}, u32[]{:S(2)}) copy-start(s32[8]{0:T(128)} %get-tuple-element.26.owners) | copy-start | bytes 100
  162.3 9.9 %all-to-all-start.8 = ((f32[16,1,512]{2,1,0:T(1,128)}), f32[16,1,512]{2,1,0:T(1,128)S(1)}, u32[]{:S(2)}, u32[]{:S(2)}) async-start(f32[16,1,512]{2,1,0:T(1,128)} %get-tuple-element.43), calls=%async_computation.8 | async-start | bytes 65536 | tf_op jit(solution)/shard_map/all_to_all | solution.py:577

commit v2 on v1

--- a/solution.py
+++ b/solution.py
@@ -87,6 +87,16 @@
     return jnp.dot(hits, both, preferred_element_type=jnp.float32)
 
 
+def square_sums(points, factor):
+    wide = points.astype(jnp.float32)
+    square = wide * wide
+    high = square.astype(jnp.bfloat16)
+    low = (square - high.astype(jnp.float32)).astype(jnp.bfloat16)
+    ones = jnp.full((8, 2 * D), 1.0, jnp.bfloat16)
+    both = jnp.concatenate([high, low], axis=1)
+    return factor * lax.dot_general(ones, both, NT, preferred_element_type=jnp.float32)[:1]
+
+
 def source_means_kernel(base, points, labels, out):
     both = totals_and_counts(one_hot(labels[...] - base[0], CL_DEV), points[...])
     counts = both[:, D:]
@@ -110,7 +120,6 @@
     for copy in copies:
         copy.start()
     acc[...] = jnp.zeros_like(acc)
-    ones = jnp.full((8, 2 * D), 1.0, jnp.bfloat16)
 
     def piece(chunk, start, points_here):
         hits = one_hot(labels[chunk] - (start + base[0]), PIECE)
@@ -129,13 +138,7 @@
                 beyond = firsts[jnp.minimum(2 * chunk + 2, 127)]
                 beyond = jnp.where(chunk < CBD - 1, beyond, N_TGT - 1)
                 most = jnp.maximum(most, (beyond - start) // PIECE)
-                wide = points.astype(jnp.float32)
-                square = wide * wide
-                high = square.astype(jnp.bfloat16)
-                low = (square - high.astype(jnp.float32)).astype(jnp.bfloat16)
-                both = jnp.concatenate([high, low], axis=1)
-                total = lax.dot_general(ones, both, NT, preferred_element_type=jnp.float32)
-                norms[chunk] = (0.5 * SCALE) * total[:1]
+                norms[chunk] = square_sums(points, 0.5 * SCALE)
             return most
 
         most = lax.fori_loop(0, 2, some, 0)
@@ -264,16 +267,13 @@
 
 def products_kernel(counts, blocks, norms, x_hbm, y_hbm, gains, halves, weights, xs, ys, sems):
     copies = start_copies(counts, blocks, x_hbm, y_hbm, xs, ys, sems)
-    mask = eye(128)
 
     def body(slot):
         x = xs[slot, :BLOCK, :]
         tail = xs[slot, BLOCK:, :].astype(jnp.float32)
+        halves[slot] = square_sums(x, 0.5)
         for h in range(2):
             at = slice(h * 128, (h + 1) * 128)
-            wide = xs[slot, at, :].astype(jnp.float32)
-            half_x = 0.5 * jnp.sum(wide * wide, axis=1, keepdims=True)
-            halves[slot, :, at] = to_row(half_x, mask)
             weights[slot, :, at] = (tail[h : h + 1] + tail[h + 2 : h + 3]) + tail[h + 4 : h + 5]
         for a in range(ACT):
             products = lax.dot_general(

time: 176 us -> 176 us (level)
  no operation moved by 1% of the time
where the time goes in v2:
time: 176 us; the launch traced here: 174 us
  blocking collectives  50.2 us (29%)
  starting transfers between devices  46.7 us (27%)
  Pallas kernels  43.4 us (25%)
  waiting for transfers between devices  27.8 us (16%)
  other arithmetic  3.19 us (2%)
    all_to_all x5, blocking collectives, exchange(): return lax.all_to_all(x, axis, split_axis=0, concat_axis=0, tiled=True)  50.2 us
    ppermute x20, starting transfers between devices, partner(): return lax.ppermute(x, axis, [(k, k ^ step) for k in range(n)])  25.8 us
    all_to_all x4, starting transfers between devices, exchange(): return lax.all_to_all(x, axis, split_axis=0, concat_axis=0, tiled=True)  20.9 us
    all_to_all x4, waiting for transfers between devices, exchange(): return lax.all_to_all(x, axis, split_axis=0, concat_axis=0, tiled=True)  18 us
    ppermute x20, waiting for transfers between devices, partner(): return lax.ppermute(x, axis, [(k, k ^ step) for k in range(n)])  9.85 us
    pallas_call x1, Pallas kernels, on_device(): call(target_stats_kernel, (vmem_shape(N_TGT, D), vmem_shape(1, N_TGT), vm...  7.34 us
    pallas_call x1, Pallas kernels, on_device(): call(second_pass_kernel, (column, column, slot_row, fine_shape), [SM, SM,...  6.62 us
    pallas_call x1, Pallas kernels, on_device(): call(adjoint_kernel, (shape(CBD, 1, BLOCK), vmem_shape(N_COLS, 1, 2 * BLO...  5.17 us
  transfers between devices with their start and end apart: 24, of which 14 were waited for; matrix products, arithmetic and copies ran while one was open for 1% of the time, Pallas kernels for 13%

profile of v2, /device:TPU:1, one launch (start us, length us, event | category | flops | bytes accessed | tf_op | source)
XLA Modules:
  0.0 173.6 jit_solution(3285611943286478632)
XLA Ops:
  0.6 2.2 %shard_map.111 = f32[16,72,128]{2,1,0:T(8,128)} custom-call(s32[1]{0:T(128)} %bitcast.5.base, bf16[2048,128]{1,0:T(8,128)(2,1)} %points.3, s32[1,2048]{1,0:T(1,128)} %bitcast.22), custom_call_target="tpu_custom_call" | custom-call | flops 100000000 | bytes 4194304 | tf_op jit(solution)/shard_map/pallas_call | solution.py:612
  2.8 8.6 %all-to-all-start = ((f32[16,72,128]{2,1,0:T(8,128)}), f32[16,72,128]{2,1,0:T(8,128)S(1)}, u32[]{:S(2)}, u32[]{:S(2)}) async-start(f32[16,72,128]{2,1,0:T(8,128)} %shard_map.111), calls=%async_computation | async-start | bytes 1179648 | tf_op jit(solution)/shard_map/all_to_all | solution.py:577
  11.4 0.9 fusion.firsts
  12.4 0.8 copy-done
  13.2 7.3 %shard_map.112 = (f32[512,128]{1,0:T(8,128)S(1)}, f32[1,512]{1,0:T(1,128)S(1)}, f32[64,1,256]{2,1,0:T(1,128)S(1)}) custom-call(s32[1]{0:T(128)} %bitcast.4.base, s32[128]{0:T(128)S(1)} %fusion.firsts, s32[64,1,256]{2,1,0:T(1,128)S(1)} %bitcast.16, bf16[16384,128]{1,0:T(8,128)(2,1)} %y_hbm.3), custom_call_target="tpu_custom_call" | custom-call | flops 1000000000 | bytes 4194304 | tf_op jit(solution)/shard_map/pallas_call | solution.py:642
  20.6 1.8 %all-to-all-done.gathered = f32[16,72,128]{2,1,0:T(8,128)S(1)} async-done(((f32[16,72,128]{2,1,0:T(8,128)}), f32[16,72,128]{2,1,0:T(8,128)S(1)}, u32[]{:S(2)}, u32[]{:S(2)}) %all-to-all-start) | async-done | bytes 589856 | tf_op jit(solution)/shard_map/all_to_all | solution.py:577
  22.4 2.0 %shard_map.113 = (f32[1024,512]{1,0:T(8,128)S(1)}, f32[8,128]{1,0:T(8,128)S(1)}, f32[16,8,128]{2,1,0:T(8,128)S(1)}) custom-call(f32[16,72,128]{2,1,0:T(8,128)S(1)} %all-to-all-done.gathered, f32[512,128]{1,0:T(8,128)S(1)} %get-tuple-element.29.targets), custom_call_target="tpu_custom_call" | custom-call | flops 1000000000 | bytes 4194304 | tf_op jit(solution)/shard_map/pallas_call | solution.py:654
  24.4 11.1 %all_to_all.45.refs_0_ = f32[16,8,128]{2,1,0:T(8,128)S(1)} all-to-all(f32[16,8,128]{2,1,0:T(8,128)S(1)} %get-tuple-element.30), channel_id=1, replica_groups=mesh['x'=4,'core'=2,'y'=4,'z'=4] {'y','z'}, dimensions={0} | all-to-all | bytes 131072 | tf_op jit(solution)/shard_map/all_to_all | solution.py:577
  35.6 0.6 shard_map.114
  36.2 2.7 %collective-permute-start = (f32[1,512]{1,0:T(1,128)S(1)}, f32[1,512]{1,0:T(1,128)S(1)}, u32[]{:S(2)}, u32[]{:S(2)}) collective-permute-start(f32[1,512]{1,0:T(1,128)S(1)} %shard_map.114), channel_id=1, source_target_pairs={{0,16},{16,0},{1,17},{17,1},{2,18},{18,2},{3,19},{19,3},{4,20},{20... | collective-permute-start | bytes 6152 | tf_op jit(solution)/shard_map/ppermute | solution.py:582
  38.9 0.8 collective-permute-done
  39.8 2.6 %collective-permute-start.3 = (f32[1,512]{1,0:T(1,128)S(1)}, f32[1,512]{1,0:T(1,128)S(1)}, u32[]{:S(2)}, u32[]{:S(2)}) collective-permute-start(f32[1,512]{1,0:T(1,128)S(1)} %multiply_add_fusion.4.refs_0_), channel_id=1, source_target_pairs={{0,96},{32,64},{64,32},{96,0},{1,97},{33,65},{65,33},{97,1},{2,98}... | collective-permute-start | bytes 6152 | tf_op jit(solution)/shard_map/ppermute | solution.py:582
  42.3 0.5 collective-permute-start.2
  42.8 0.3 collective-permute-start.1
  43.1 0.4 collective-permute-done.3.refs_3_
  43.5 2.8 %collective-permute-done.2.refs_2_ = f32[1,512]{1,0:T(1,128)S(1)} collective-permute-done((f32[1,512]{1,0:T(1,128)S(1)}, f32[1,512]{1,0:T(1,128)S(1)}, u32[]{:S(2)}, u32[]{:S(2)}) %collective-permute-start.2) | collective-permute-done | bytes 2080 | tf_op jit(solution)/shard_map/ppermute | solution.py:582
  46.3 0.6 shard_map.115
  46.9 9.5 %all_to_all.46.refs_0_ = f32[16,8,128]{2,1,0:T(8,128)S(1)} all-to-all(f32[16,8,128]{2,1,0:T(8,128)S(1)} %shard_map.115), channel_id=1, replica_groups=mesh['x'=4,'core'=2,'y'=4,'z'=4] {'y','z'}, dimensions={0} | all-to-all | bytes 131072 | tf_op jit(solution)/shard_map/all_to_all | solution.py:577
  56.4 0.6 shard_map.116
  57.0 10.9 %all_to_all.47.refs_0_ = f32[8,1,512]{2,1,0:T(1,128)S(1)} all-to-all(f32[8,1,512]{2,1,0:T(1,128)S(1)} %shard_map.116), channel_id=1, replica_groups=mesh['x'=4,'core'=2,'y'=4,'z'=4] {'x','core'}, dimensions={0} | all-to-all | bytes 32768 | tf_op jit(solution)/shard_map/all_to_all | solution.py:577
  67.9 0.6 shard_map.117
  68.5 9.5 %all_to_all.48.refs_0_ = f32[16,8,128]{2,1,0:T(8,128)S(1)} all-to-all(f32[16,8,128]{2,1,0:T(8,128)S(1)} %shard_map.117), channel_id=1, replica_groups=mesh['x'=4,'core'=2,'y'=4,'z'=4] {'y','z'}, dimensions={0} | all-to-all | bytes 131072 | tf_op jit(solution)/shard_map/all_to_all | solution.py:577
  78.0 0.6 shard_map.118
  78.6 9.1 %all_to_all.49.refs_0_ = f32[8,1,512]{2,1,0:T(1,128)S(1)} all-to-all(f32[8,1,512]{2,1,0:T(1,128)S(1)} %shard_map.118), channel_id=1, replica_groups=mesh['x'=4,'core'=2,'y'=4,'z'=4] {'x','core'}, dimensions={0} | all-to-all | bytes 32768 | tf_op jit(solution)/shard_map/all_to_all | solution.py:577
  87.7 1.3 shard_map.119
  89.0 3.5 %all-to-all-start.6 = ((f32[16,8,128]{2,1,0:T(8,128)}), f32[16,8,128]{2,1,0:T(8,128)S(1)}, u32[]{:S(2)}, u32[]{:S(2)}) async-start(f32[16,8,128]{2,1,0:T(8,128)} %shard_map.119), calls=%async_computation.6 | async-start | bytes 131072 | tf_op jit(solution)/shard_map/all_to_all | solution.py:577
  92.5 2.3 %plan.1 = (s32[16]{0:T(128)}, s32[64]{0:T(128)}, s32[8]{0:T(128)}) custom-call(s32[1]{0:T(128)} %bitcast.row, s32[1]{0:T(128)} %bitcast.1.col, s32[4,1024]{1,0:T(4,128)} %bitcast.21, s32[8,128]{1,0:T(8,128)} %bitcast.24), custom_call_target="tpu_custom_call" | custom-call | tf_op jit(solution)/shard_map/plan/pallas_call | solution.py:619
  94.8 0.7 copy-done.5
  95.5 2.1 %shard_map.121 = bf16[16,272,128]{2,1,0:T(8,128)(2,1)} custom-call(s32[8]{0:T(128)S(1)} %copy-done.5, bf16[2048,128]{1,0:T(8,128)(2,1)} %points.3, f32[8,2,128]{2,1,0:T(2,128)} %bitcast.23), custom_call_target="tpu_custom_call" | custom-call | flops 100000000 | bytes 4194304 | tf_op jit(solution)/shard_map/pallas_call | solution.py:636
  97.6 1.3 all-to-all-done.6.refs_0_
  98.9 5.3 %all-to-all-start.7 = ((bf16[16,272,128]{2,1,0:T(8,128)(2,1)}), bf16[16,272,128]{2,1,0:T(8,128)(2,1)}, u32[]{:S(2)}, u32[]{:S(2)}) async-start(bf16[16,272,128]{2,1,0:T(8,128)(2,1)} %shard_map.121), calls=%async_computation.7 | async-start | bytes 2228224 | tf_op jit(solution)/shard_map/all_to_all | solution.py:577
  104.3 0.6 shard_map.120
  104.9 1.5 collective-permute-start.4
  106.4 0.8 collective-permute-done.4
  107.2 1.0 collective-permute-start.7
  108.2 1.2 collective-permute-start.6
  109.4 1.2 collective-permute-start.5
  110.6 9.9 %all-to-all-done.7.x_hbm = bf16[16,272,128]{2,1,0:T(8,128)(2,1)} async-done(((bf16[16,272,128]{2,1,0:T(8,128)(2,1)}), bf16[16,272,128]{2,1,0:T(8,128)(2,1)}, u32[]{:S(2)}, u32[]{:S(2)}) %all-to-all-start.7) | async-done | bytes 1114144 | tf_op jit(solution)/shard_map/all_to_all | solution.py:577
  120.5 5.1 %shard_map.122 = (f32[16,256,1024]{2,1,0:T(8,128)S(1)}, f32[16,1,256]{2,1,0:T(1,128)S(1)}, f32[16,1,256]{2,1,0:T(1,128)S(1)}) custom-call(s32[16]{0:T(128)S(1)} %copy-done.3, s32[64]{0:T(128)S(1)} %copy-done.4, f32[64,1,256]{2,1,0:T(1,128)S(1)} %get-tuple-element.34.norms, bf16[16,272,128]{2,1,0:T(8,128)(2,1)} %all-to-all-done.7.x_hbm, bf16[16384,128]{1,0:T(8,128)(2,1)} %y_hbm.3), custom_call_target="tpu_custom_call" | custom-call | flops 1000000000 | bytes 4194304 | tf_op jit(solution)/shard_map/pallas_call | solution.py:689
  125.6 4.5 %shard_map.123 = (f32[64,1,256]{2,1,0:T(1,128)S(1)}, f32[16,256,1024]{2,1,0:T(8,128)S(1)}) custom-call(s32[1]{0:T(128)} %bitcast.4.base, s32[16]{0:T(128)S(1)} %copy-done.3, s32[64]{0:T(128)S(1)} %copy-done.4, f32[1,512]{1,0:T(1,128)S(1)} %multiply_add_fusion.3.p0, f32[1,512]{1,0:T(1,128)S(1)} %collective-permute-done.5.p1, ...), custom_call_target="tpu_custom_call", output_to_operand_aliasing={{1}: (8, {})} | custom-call | flops 100000000 | bytes 4194304 | tf_op jit(solution)/shard_map/pallas_call | solution.py:710
  130.1 3.3 %collective-permute-start.8 = (f32[64,1,256]{2,1,0:T(1,128)S(1)}, f32[64,1,256]{2,1,0:T(1,128)S(1)}, u32[]{:S(2)}, u32[]{:S(2)}) collective-permute-start(f32[64,1,256]{2,1,0:T(1,128)S(1)} %get-tuple-element.36), channel_id=1, source_target_pairs={{0,16},{16,0},{1,17},{17,1},{2,18},{18,2},{3,19},{19,3},{4,20},{20... | collective-permute-start | bytes 196616 | tf_op jit(solution)/shard_map/ppermute | solution.py:582
  133.4 0.9 collective-permute-done.8
  134.6 1.0 collective-permute-start.11
  135.5 1.2 collective-permute-start.10
  136.7 1.1 collective-permute-start.9
  137.9 1.1 collective-permute-done.11.l3
  139.0 1.3 collective-permute-done.10.l2
  140.3 0.6 collective-permute-done.9.l1
  140.8 6.6 %shard_map.124 = (f32[64,1,256]{2,1,0:T(1,128)S(1)}, f32[64,1,256]{2,1,0:T(1,128)S(1)}, f32[16,1,256]{2,1,0:T(1,128)S(1)}, f32[16,256,1024]{2,1,0:T(8,128)S(1)}) custom-call(s32[16]{0:T(128)S(1)} %copy-done.3, s32[64]{0:T(128)S(1)} %copy-done.4, f32[64,1,256]{2,1,0:T(1,128)S(1)} %multiply_add_fusion.2.l0, ...), custom_call_target="tpu_custom_call", output_to_operand_aliasing={{3}: (7, {})} | custom-call | flops 100000000 | bytes 4194304 | tf_op jit(solution)/shard_map/pallas_call | solution.py:726
  147.5 1.6 collective-permute-start.12
  149.1 0.8 collective-permute-done.12
  149.9 0.4 collective-permute-done.16
  150.3 0.4 multiply_add_fusion
  150.7 1.8 %collective-permute-start.15 = (f32[64,1,256]{2,1,0:T(1,128)S(1)}, f32[64,1,256]{2,1,0:T(1,128)S(1)}, u32[]{:S(2)}, u32[]{:S(2)}) collective-permute-start(f32[64,1,256]{2,1,0:T(1,128)S(1)} %get-tuple-element.49.l0), channel_id=1, source_target_pairs={{0,96},{32,64},{64,32},{96,0},{1,97},{33,65},{65,33},{97,1},{2,98}... | collective-permute-start | bytes 196616 | tf_op jit(solution)/shard_map/ppermute | solution.py:582
  152.5 0.8 collective-permute-start.14
  153.4 0.7 collective-permute-start.13
  154.1 1.7 collective-permute-start.19
  155.8 0.8 collective-permute-start.18
  156.6 0.7 collective-permute-start.17
  157.3 5.2 %shard_map.125 = (f32[64,1,256]{2,1,0:T(1,128)}, f32[16,1,512]{2,1,0:T(1,128)}) custom-call(s32[16]{0:T(128)S(1)} %copy-done.3, s32[64]{0:T(128)S(1)} %copy-done.4, f32[64,1,256]{2,1,0:T(1,128)S(1)} %get-tuple-element.49.l0, f32[64,1,256]{2,1,0:T(1,128)S(1)} %collective-permute-done.13.l1, f32[64,1,256]{2,1,0:T(1,128)S(1)} %collective-permute-done.14.l2, ...), custom_call_target="tpu_custom_call" | custom-call | flops 100000000 | bytes 4194304 | tf_op jit(solution)/shard_map/pallas_call | solution.py:740
  162.5 3.5 %all-to-all-start.8 = ((f32[16,1,512]{2,1,0:T(1,128)}), f32[16,1,512]{2,1,0:T(1,128)S(1)}, u32[]{:S(2)}, u32[]{:S(2)}) async-start(f32[16,1,512]{2,1,0:T(1,128)} %get-tuple-element.43), calls=%async_computation.8 | async-start | bytes 65536 | tf_op jit(solution)/shard_map/all_to_all | solution.py:577
  166.0 1.5 add_add_fusion
  167.5 4.9 %all-to-all-done.8.back = f32[16,1,512]{2,1,0:T(1,128)S(1)} async-done(((f32[16,1,512]{2,1,0:T(1,128)}), f32[16,1,512]{2,1,0:T(1,128)S(1)}, u32[]{:S(2)}, u32[]{:S(2)}) %all-to-all-start.8) | async-done | bytes 32800 | tf_op jit(solution)/shard_map/all_to_all | solution.py:577
  172.4 1.2 shard_map.126
  (26 shorter events, 0.4 us)
Async XLA Ops:
  2.8 19.6 %all-to-all-start = ((f32[16,72,128]{2,1,0:T(8,128)}), f32[16,72,128]{2,1,0:T(8,128)S(1)}, u32[]{:S(2)}, u32[]{:S(2)}) async-start(f32[16,72,128]{2,1,0:T(8,128)} %shard_map.111), calls=%async_computation | async-start | bytes 1179648 | tf_op jit(solution)/shard_map/all_to_all | solution.py:577
  12.4 0.8 copy-start
  36.2 3.6 %collective-permute-start = (f32[1,512]{1,0:T(1,128)S(1)}, f32[1,512]{1,0:T(1,128)S(1)}, u32[]{:S(2)}, u32[]{:S(2)}) collective-permute-start(f32[1,512]{1,0:T(1,128)S(1)} %shard_map.114), channel_id=1, source_target_pairs={{0,16},{16,0},{1,17},{17,1},{2,18},{18,2},{3,19},{19,3},{4,20},{20... | collective-permute-start | bytes 6152 | tf_op jit(solution)/shard_map/ppermute | solution.py:582
  39.8 3.7 %collective-permute-start.3 = (f32[1,512]{1,0:T(1,128)S(1)}, f32[1,512]{1,0:T(1,128)S(1)}, u32[]{:S(2)}, u32[]{:S(2)}) collective-permute-start(f32[1,512]{1,0:T(1,128)S(1)} %multiply_add_fusion.4.refs_0_), channel_id=1, source_target_pairs={{0,96},{32,64},{64,32},{96,0},{1,97},{33,65},{65,33},{97,1},{2,98}... | collective-permute-start | bytes 6152 | tf_op jit(solution)/shard_map/ppermute | solution.py:582
  42.3 3.9 %collective-permute-start.2 = (f32[1,512]{1,0:T(1,128)S(1)}, f32[1,512]{1,0:T(1,128)S(1)}, u32[]{:S(2)}, u32[]{:S(2)}) collective-permute-start(f32[1,512]{1,0:T(1,128)S(1)} %multiply_add_fusion.4.refs_0_), channel_id=1, source_target_pairs={{0,64},{32,96},{64,0},{96,32},{1,65},{33,97},{65,1},{97,33},{2,66}... | collective-permute-start | bytes 6152 | tf_op jit(solution)/shard_map/ppermute | solution.py:582
  42.8 3.4 %collective-permute-start.1 = (f32[1,512]{1,0:T(1,128)S(1)}, f32[1,512]{1,0:T(1,128)S(1)}, u32[]{:S(2)}, u32[]{:S(2)}) collective-permute-start(f32[1,512]{1,0:T(1,128)S(1)} %multiply_add_fusion.4.refs_0_), channel_id=1, source_target_pairs={{0,32},{32,0},{64,96},{96,64},{1,33},{33,1},{65,97},{97,65},{2,34}... | collective-permute-start | bytes 6152 | tf_op jit(solution)/shard_map/ppermute | solution.py:582
  89.0 10.0 %all-to-all-start.6 = ((f32[16,8,128]{2,1,0:T(8,128)}), f32[16,8,128]{2,1,0:T(8,128)S(1)}, u32[]{:S(2)}, u32[]{:S(2)}) async-start(f32[16,8,128]{2,1,0:T(8,128)} %shard_map.119), calls=%async_computation.6 | async-start | bytes 131072 | tf_op jit(solution)/shard_map/all_to_all | solution.py:577
  94.8 25.7 %copy-start.3 = (s32[16]{0:T(128)S(1)}, s32[16]{0:T(128)}, u32[]{:S(2)}) copy-start(s32[16]{0:T(128)} %get-tuple-element.27.counts) | copy-start | bytes 196
  94.8 25.7 %copy-start.4 = (s32[64]{0:T(128)S(1)}, s32[64]{0:T(128)}, u32[]{:S(2)}) copy-start(s32[64]{0:T(128)} %get-tuple-element.28.blocks) | copy-start | bytes 772
  94.8 0.7 copy-start.5
  98.9 21.6 %all-to-all-start.7 = ((bf16[16,272,128]{2,1,0:T(8,128)(2,1)}), bf16[16,272,128]{2,1,0:T(8,128)(2,1)}, u32[]{:S(2)}, u32[]{:S(2)}) async-start(bf16[16,272,128]{2,1,0:T(8,128)(2,1)} %shard_map.121), calls=%async_computation.7 | async-start | bytes 2228224 | tf_op jit(solution)/shard_map/all_to_all | solution.py:577
  104.3 21.4 %copy-start.1 = (s32[16384]{0:T(1024)S(1)}, s32[16384]{0:T(1024)}, u32[]{:S(2)}) copy-start(s32[16384]{0:T(1024)} %param.11) | copy-start | bytes 196612
  104.9 2.4 %collective-permute-start.4 = (f32[1,512]{1,0:T(1,128)S(1)}, f32[1,512]{1,0:T(1,128)S(1)}, u32[]{:S(2)}, u32[]{:S(2)}) collective-permute-start(f32[1,512]{1,0:T(1,128)S(1)} %shard_map.120), channel_id=1, source_target_pairs={{0,16},{16,0},{1,17},{17,1},{2,18},{18,2},{3,19},{19,3},{4,20},{20... | collective-permute-start | bytes 6152 | tf_op jit(solution)/shard_map/ppermute | solution.py:582
  107.2 18.4 %collective-permute-start.7 = (f32[1,512]{1,0:T(1,128)S(1)}, f32[1,512]{1,0:T(1,128)S(1)}, u32[]{:S(2)}, u32[]{:S(2)}) collective-permute-start(f32[1,512]{1,0:T(1,128)S(1)} %multiply_add_fusion.3.p0), channel_id=1, source_target_pairs={{0,96},{32,64},{64,32},{96,0},{1,97},{33,65},{65,33},{97,1},{2,98}... | collective-permute-start | bytes 6152 | tf_op jit(solution)/shard_map/ppermute | solution.py:582
  108.2 17.4 %collective-permute-start.6 = (f32[1,512]{1,0:T(1,128)S(1)}, f32[1,512]{1,0:T(1,128)S(1)}, u32[]{:S(2)}, u32[]{:S(2)}) collective-permute-start(f32[1,512]{1,0:T(1,128)S(1)} %multiply_add_fusion.3.p0), channel_id=1, source_target_pairs={{0,64},{32,96},{64,0},{96,32},{1,65},{33,97},{65,1},{97,33},{2,66}... | collective-permute-start | bytes 6152 | tf_op jit(solution)/shard_map/ppermute | solution.py:582
  109.4 16.2 %collective-permute-start.5 = (f32[1,512]{1,0:T(1,128)S(1)}, f32[1,512]{1,0:T(1,128)S(1)}, u32[]{:S(2)}, u32[]{:S(2)}) collective-permute-start(f32[1,512]{1,0:T(1,128)S(1)} %multiply_add_fusion.3.p0), channel_id=1, source_target_pairs={{0,32},{32,0},{64,96},{96,64},{1,33},{33,1},{65,97},{97,65},{2,34}... | collective-permute-start | bytes 6152 | tf_op jit(solution)/shard_map/ppermute | solution.py:582
  130.1 4.2 %collective-permute-start.8 = (f32[64,1,256]{2,1,0:T(1,128)S(1)}, f32[64,1,256]{2,1,0:T(1,128)S(1)}, u32[]{:S(2)}, u32[]{:S(2)}) collective-permute-start(f32[64,1,256]{2,1,0:T(1,128)S(1)} %get-tuple-element.36), channel_id=1, source_target_pairs={{0,16},{16,0},{1,17},{17,1},{2,18},{18,2},{3,19},{19,3},{4,20},{20... | collective-permute-start | bytes 196616 | tf_op jit(solution)/shard_map/ppermute | solution.py:582
  134.6 4.4 %collective-permute-start.11 = (f32[64,1,256]{2,1,0:T(1,128)S(1)}, f32[64,1,256]{2,1,0:T(1,128)S(1)}, u32[]{:S(2)}, u32[]{:S(2)}) collective-permute-start(f32[64,1,256]{2,1,0:T(1,128)S(1)} %multiply_add_fusion.2.l0), channel_id=1, source_target_pairs={{0,96},{32,64},{64,32},{96,0},{1,97},{33,65},{65,33},{97,1},{2,98}... | collective-permute-start | bytes 196616 | tf_op jit(solution)/shard_map/ppermute | solution.py:582
  135.5 4.7 %collective-permute-start.10 = (f32[64,1,256]{2,1,0:T(1,128)S(1)}, f32[64,1,256]{2,1,0:T(1,128)S(1)}, u32[]{:S(2)}, u32[]{:S(2)}) collective-permute-start(f32[64,1,256]{2,1,0:T(1,128)S(1)} %multiply_add_fusion.2.l0), channel_id=1, source_target_pairs={{0,64},{32,96},{64,0},{96,32},{1,65},{33,97},{65,1},{97,33},{2,66}... | collective-permute-start | bytes 196616 | tf_op jit(solution)/shard_map/ppermute | solution.py:582
  136.7 4.1 %collective-permute-start.9 = (f32[64,1,256]{2,1,0:T(1,128)S(1)}, f32[64,1,256]{2,1,0:T(1,128)S(1)}, u32[]{:S(2)}, u32[]{:S(2)}) collective-permute-start(f32[64,1,256]{2,1,0:T(1,128)S(1)} %multiply_add_fusion.2.l0), channel_id=1, source_target_pairs={{0,32},{32,0},{64,96},{96,64},{1,33},{33,1},{65,97},{97,65},{2,34}... | collective-permute-start | bytes 196616 | tf_op jit(solution)/shard_map/ppermute | solution.py:582
  140.8 16.5 %copy-start.2 = (f32[16384]{0:T(1024)S(1)}, f32[16384]{0:T(1024)}, u32[]{:S(2)}) copy-start(f32[16384]{0:T(1024)} %param.15) | copy-start | bytes 196612
  147.5 2.5 %collective-permute-start.12 = (f32[64,1,256]{2,1,0:T(1,128)S(1)}, f32[64,1,256]{2,1,0:T(1,128)S(1)}, u32[]{:S(2)}, u32[]{:S(2)}) collective-permute-start(f32[64,1,256]{2,1,0:T(1,128)S(1)} %get-tuple-element.39), channel_id=1, source_target_pairs={{0,16},{16,0},{1,17},{17,1},{2,18},{18,2},{3,19},{19,3},{4,20},{20... | collective-permute-start | bytes 196616 | tf_op jit(solution)/shard_map/ppermute | solution.py:582
  149.0 1.3 collective-permute-start.16
  150.7 5.9 %collective-permute-start.15 = (f32[64,1,256]{2,1,0:T(1,128)S(1)}, f32[64,1,256]{2,1,0:T(1,128)S(1)}, u32[]{:S(2)}, u32[]{:S(2)}) collective-permute-start(f32[64,1,256]{2,1,0:T(1,128)S(1)} %get-tuple-element.49.l0), channel_id=1, source_target_pairs={{0,96},{32,64},{64,32},{96,0},{1,97},{33,65},{65,33},{97,1},{2,98}... | collective-permute-start | bytes 196616 | tf_op jit(solution)/shard_map/ppermute | solution.py:582
  152.5 4.8 %collective-permute-start.14 = (f32[64,1,256]{2,1,0:T(1,128)S(1)}, f32[64,1,256]{2,1,0:T(1,128)S(1)}, u32[]{:S(2)}, u32[]{:S(2)}) collective-permute-start(f32[64,1,256]{2,1,0:T(1,128)S(1)} %get-tuple-element.49.l0), channel_id=1, source_target_pairs={{0,64},{32,96},{64,0},{96,32},{1,65},{33,97},{65,1},{97,33},{2,66}... | collective-permute-start | bytes 196616 | tf_op jit(solution)/shard_map/ppermute | solution.py:582
  153.4 4.0 %collective-permute-start.13 = (f32[64,1,256]{2,1,0:T(1,128)S(1)}, f32[64,1,256]{2,1,0:T(1,128)S(1)}, u32[]{:S(2)}, u32[]{:S(2)}) collective-permute-start(f32[64,1,256]{2,1,0:T(1,128)S(1)} %get-tuple-element.49.l0), channel_id=1, source_target_pairs={{0,32},{32,0},{64,96},{96,64},{1,33},{33,1},{65,97},{97,65},{2,34}... | collective-permute-start | bytes 196616 | tf_op jit(solution)/shard_map/ppermute | solution.py:582
  154.1 11.9 %collective-permute-start.19 = (f32[64,1,256]{2,1,0:T(1,128)S(1)}, f32[64,1,256]{2,1,0:T(1,128)S(1)}, u32[]{:S(2)}, u32[]{:S(2)}) collective-permute-start(f32[64,1,256]{2,1,0:T(1,128)S(1)} %get-tuple-element.48), channel_id=1, source_target_pairs={{0,96},{32,64},{64,32},{96,0},{1,97},{33,65},{65,33},{97,1},{2,98}... | collective-permute-start | bytes 196616 | tf_op jit(solution)/shard_map/ppermute | solution.py:582
  155.8 10.2 %collective-permute-start.18 = (f32[64,1,256]{2,1,0:T(1,128)S(1)}, f32[64,1,256]{2,1,0:T(1,128)S(1)}, u32[]{:S(2)}, u32[]{:S(2)}) collective-permute-start(f32[64,1,256]{2,1,0:T(1,128)S(1)} %get-tuple-element.48), channel_id=1, source_target_pairs={{0,64},{32,96},{64,0},{96,32},{1,65},{33,97},{65,1},{97,33},{2,66}... | collective-permute-start | bytes 196616 | tf_op jit(solution)/shard_map/ppermute | solution.py:582
  156.6 9.4 %collective-permute-start.17 = (f32[64,1,256]{2,1,0:T(1,128)S(1)}, f32[64,1,256]{2,1,0:T(1,128)S(1)}, u32[]{:S(2)}, u32[]{:S(2)}) collective-permute-start(f32[64,1,256]{2,1,0:T(1,128)S(1)} %get-tuple-element.48), channel_id=1, source_target_pairs={{0,32},{32,0},{64,96},{96,64},{1,33},{33,1},{65,97},{97,65},{2,34}... | collective-permute-start | bytes 196616 | tf_op jit(solution)/shard_map/ppermute | solution.py:582
  157.3 15.1 %copy-start.6 = (s32[8]{0:T(128)S(1)}, s32[8]{0:T(128)}, u32[]{:S(2)}) copy-start(s32[8]{0:T(128)} %get-tuple-element.26.owners) | copy-start | bytes 100
  162.5 9.9 %all-to-all-start.8 = ((f32[16,1,512]{2,1,0:T(1,128)}), f32[16,1,512]{2,1,0:T(1,128)S(1)}, u32[]{:S(2)}, u32[]{:S(2)}) async-start(f32[16,1,512]{2,1,0:T(1,128)} %get-tuple-element.43), calls=%async_computation.8 | async-start | bytes 65536 | tf_op jit(solution)/shard_map/all_to_all | solution.py:577

commit v3 on v2

--- a/solution.py
+++ b/solution.py
@@ -265,7 +265,7 @@
     return copies
 
 
-def products_kernel(counts, blocks, norms, x_hbm, y_hbm, gains, halves, weights, xs, ys, sems):
+def products_kernel(counts, blocks, order, norms, x_hbm, y_hbm, gains, halves, weights, xs, ys, sems):
     copies = start_copies(counts, blocks, x_hbm, y_hbm, xs, ys, sems)
 
     def body(slot):
@@ -283,7 +283,7 @@
                 SCALE * products - norms[blocks[slot * ACT + a]]
             )
 
-    each_slot(counts, body, copies)
+    slot_pairs(order, body, copies)
 
 
 def slot_potential(slot, counts, blocks, values):
@@ -421,6 +421,27 @@
             lam_out[slot, :, at] = to_row(jnp.concatenate(lams[h * CHUNKS // 2 : (h + 1) * CHUNKS // 2], axis=0), mask)
 
 
+def slot_pairs(order, body, copies=None):
+    used = order[N_COLS + 1]
+
+    def step(pair, carry):
+        first, second = order[2 * pair], order[2 * pair + 1]
+        if copies is not None:
+            for copy in copies(first):
+                copy.wait()
+
+            @pl.when(2 * pair + 1 < used)
+            def _():
+                for copy in copies(second):
+                    copy.wait()
+
+        body(first)
+        body(second)
+        return carry
+
+    lax.fori_loop(0, (used + 1) // 2, step, 0)
+
+
 def clear(best, mixed=None):
     best[...] = jnp.full(best.shape, lowest, jnp.float32)
     if mixed is not None:
@@ -467,7 +488,7 @@
 
 
 def adjoint_kernel(
-    counts, blocks, l0, l1, l2, l3, lam, halves, weights, col_weights, gains,
+    counts, blocks, order, l0, l1, l2, l3, lam, halves, weights, col_weights, gains,
     potential_out, back, values,
 ):
     total = lse_list([l0[...], l1[...], l2[...], l3[...]])
@@ -498,10 +519,12 @@
                 weights[slot, :, half] * mass + cross
             )
 
-    each_slot(counts, body)
-
-
-def plan_kernel(row, col, lists_hbm, counts_hbm, counts, blocks, owners, lists, found, sems):
+    slot_pairs(order, body)
+
+
+def plan_kernel(
+    row, col, lists_hbm, counts_hbm, counts, blocks, owners, order, lists, found, sems
+):
     first = pl.multiple_of(row[0] * 128, 128)
     copies = [
         pltpu.make_async_copy(lists_hbm.at[:, pl.ds(first, 128)], lists, sems.at[0]),
@@ -514,7 +537,7 @@
     for q in range(RBD):
         owners[q] = lists[0, col[0] * RBD + q] >> 6
 
-    def fill(slot, carry):
+    def fill(slot, place):
         count = jnp.int32(0)
         chosen = [jnp.int32(0)] * ACT
         for q in range(RBD):
@@ -527,9 +550,12 @@
         counts[slot] = count
         for a in range(ACT):
             blocks[slot * ACT + a] = chosen[a]
-        return carry
-
-    lax.fori_loop(0, N_COLS, fill, 0)
+        order[place] = slot
+        return place + jnp.where(count > 0, 1, 0)
+
+    used = lax.fori_loop(0, N_COLS, fill, jnp.int32(0))
+    order[used] = order[jnp.maximum(used - 1, 0)]
+    order[N_COLS + 1] = used
 
 
 def home_kernel(owners, back, potential, adjoint):
@@ -616,11 +642,13 @@
 
     row_weights = row_weight.reshape(RBD, 2, 128)
     col_weights = col_weight.reshape(CBD, 1, BLOCK)
-    counts, blocks, owners = pl.pallas_call(
+    counts, blocks, owners, order = pl.pallas_call(
         plan_kernel,
-        out_shape=tuple(jax.ShapeDtypeStruct((n,), jnp.int32) for n in (N_COLS, N_COLS * ACT, RBD)),
+        out_shape=tuple(
+            jax.ShapeDtypeStruct((n,), jnp.int32) for n in (N_COLS, N_COLS * ACT, RBD, N_COLS + 2)
+        ),
         in_specs=[SM, SM, ANY, ANY],
-        out_specs=(SM, SM, SM),
+        out_specs=(SM, SM, SM, SM),
         scratch_shapes=[
             pltpu.SMEM((ACT, 128), jnp.int32),
             pltpu.SMEM((128,), jnp.int32),
@@ -689,14 +717,14 @@
     fine_gains, halves, weights = call(
         products_kernel,
         (vmem_shape(N_COLS, BLOCK, WIDTH), slot_row, slot_row),
-        [SM, SM, VM, ANY, ANY],
+        [SM, SM, SM, VM, ANY, ANY],
         [
             pltpu.VMEM((N_COLS, PACKED, D), jnp.bfloat16),
             pltpu.VMEM((N_COLS * ACT, BLOCK, D), jnp.bfloat16),
             pltpu.SemaphoreType.DMA((N_COLS, ACT + 1)),
         ],
         flops=1e9,
-    )(counts, blocks, in_vmem(norms), in_hbm(points_here), in_hbm(target_points))
+    )(counts, blocks, order, in_vmem(norms), in_hbm(points_here), in_hbm(target_points))
     fine_gains, halves, weights = in_vmem(fine_gains), in_vmem(halves), in_vmem(weights)
     column = vmem_shape(CBD, 1, BLOCK)
     values_scratch = pltpu.VMEM((CBD, 1, BLOCK), jnp.float32)
@@ -740,10 +768,10 @@
     col_potential, back = call(
         adjoint_kernel,
         (shape(CBD, 1, BLOCK), vmem_shape(N_COLS, 1, 2 * BLOCK)),
-        [SM, SM, VM, VM, VM, VM, VM, VM, VM, VM, VM],
+        [SM, SM, SM, VM, VM, VM, VM, VM, VM, VM, VM, VM],
         [values_scratch],
     )(
-        counts, blocks, *[in_vmem(part) for part in best_parts], in_vmem(lam), halves,
+        counts, blocks, order, *[in_vmem(part) for part in best_parts], in_vmem(lam), halves,
         weights, col_weights, in_vmem(fine_gains),
     )
     total = lse_list(best_parts)

time: 176 us -> 175 us (level)
  no operation moved by 1% of the time
where the time goes in v3:
time: 175 us; the launch traced here: 173 us
  blocking collectives  50.2 us (29%)
  starting transfers between devices  46.9 us (27%)
  Pallas kernels  42.5 us (24%)
  waiting for transfers between devices  27.8 us (16%)
  other arithmetic  3.19 us (2%)
    all_to_all x5, blocking collectives, exchange(): return lax.all_to_all(x, axis, split_axis=0, concat_axis=0, tiled=True)  50.2 us
    ppermute x20, starting transfers between devices, partner(): return lax.ppermute(x, axis, [(k, k ^ step) for k in range(n)])  26 us
    all_to_all x4, starting transfers between devices, exchange(): return lax.all_to_all(x, axis, split_axis=0, concat_axis=0, tiled=True)  20.9 us
    all_to_all x4, waiting for transfers between devices, exchange(): return lax.all_to_all(x, axis, split_axis=0, concat_axis=0, tiled=True)  18 us
    ppermute x20, waiting for transfers between devices, partner(): return lax.ppermute(x, axis, [(k, k ^ step) for k in range(n)])  9.85 us
    pallas_call x1, Pallas kernels, on_device(): call(target_stats_kernel, (vmem_shape(N_TGT, D), vmem_shape(1, N_TGT), vm...  7.34 us
    pallas_call x1, Pallas kernels, on_device(): call(second_pass_kernel, (column, column, slot_row, fine_shape), [SM, SM,...  6.62 us
    pallas_call x1, Pallas kernels, on_device(): call(adjoint_kernel, (shape(CBD, 1, BLOCK), vmem_shape(N_COLS, 1, 2 * BLO...  4.9 us
  transfers between devices with their start and end apart: 24, of which 14 were waited for; matrix products, arithmetic and copies ran while one was open for 1% of the time, Pallas kernels for 13%

profile of v3, /device:TPU:1, one launch (start us, length us, event | category | flops | bytes accessed | tf_op | source)
XLA Modules:
  0.0 172.9 jit_solution(12682510494568592852)
XLA Ops:
  0.6 2.2 %shard_map.111 = f32[16,72,128]{2,1,0:T(8,128)} custom-call(s32[1]{0:T(128)} %bitcast.5.base, bf16[2048,128]{1,0:T(8,128)(2,1)} %points.3, s32[1,2048]{1,0:T(1,128)} %bitcast.22), custom_call_target="tpu_custom_call" | custom-call | flops 100000000 | bytes 4194304 | tf_op jit(solution)/shard_map/pallas_call | solution.py:638
  2.8 8.6 %all-to-all-start = ((f32[16,72,128]{2,1,0:T(8,128)}), f32[16,72,128]{2,1,0:T(8,128)S(1)}, u32[]{:S(2)}, u32[]{:S(2)}) async-start(f32[16,72,128]{2,1,0:T(8,128)} %shard_map.111), calls=%async_computation | async-start | bytes 1179648 | tf_op jit(solution)/shard_map/all_to_all | solution.py:603
  11.4 0.9 fusion.firsts
  12.4 0.8 copy-done
  13.2 7.3 %shard_map.112 = (f32[512,128]{1,0:T(8,128)S(1)}, f32[1,512]{1,0:T(1,128)S(1)}, f32[64,1,256]{2,1,0:T(1,128)S(1)}) custom-call(s32[1]{0:T(128)} %bitcast.4.base, s32[128]{0:T(128)S(1)} %fusion.firsts, s32[64,1,256]{2,1,0:T(1,128)S(1)} %bitcast.16, bf16[16384,128]{1,0:T(8,128)(2,1)} %y_hbm.3), custom_call_target="tpu_custom_call" | custom-call | flops 1000000000 | bytes 4194304 | tf_op jit(solution)/shard_map/pallas_call | solution.py:670
  20.6 1.8 %all-to-all-done.gathered = f32[16,72,128]{2,1,0:T(8,128)S(1)} async-done(((f32[16,72,128]{2,1,0:T(8,128)}), f32[16,72,128]{2,1,0:T(8,128)S(1)}, u32[]{:S(2)}, u32[]{:S(2)}) %all-to-all-start) | async-done | bytes 589856 | tf_op jit(solution)/shard_map/all_to_all | solution.py:603
  22.4 2.0 %shard_map.113 = (f32[1024,512]{1,0:T(8,128)S(1)}, f32[8,128]{1,0:T(8,128)S(1)}, f32[16,8,128]{2,1,0:T(8,128)S(1)}) custom-call(f32[16,72,128]{2,1,0:T(8,128)S(1)} %all-to-all-done.gathered, f32[512,128]{1,0:T(8,128)S(1)} %get-tuple-element.31.targets), custom_call_target="tpu_custom_call" | custom-call | flops 1000000000 | bytes 4194304 | tf_op jit(solution)/shard_map/pallas_call | solution.py:682
  24.5 11.1 %all_to_all.45.refs_0_ = f32[16,8,128]{2,1,0:T(8,128)S(1)} all-to-all(f32[16,8,128]{2,1,0:T(8,128)S(1)} %get-tuple-element.32), channel_id=1, replica_groups=mesh['x'=4,'core'=2,'y'=4,'z'=4] {'y','z'}, dimensions={0} | all-to-all | bytes 131072 | tf_op jit(solution)/shard_map/all_to_all | solution.py:603
  35.6 0.6 shard_map.114
  36.2 2.7 %collective-permute-start = (f32[1,512]{1,0:T(1,128)S(1)}, f32[1,512]{1,0:T(1,128)S(1)}, u32[]{:S(2)}, u32[]{:S(2)}) collective-permute-start(f32[1,512]{1,0:T(1,128)S(1)} %shard_map.114), channel_id=1, source_target_pairs={{0,16},{16,0},{1,17},{17,1},{2,18},{18,2},{3,19},{19,3},{4,20},{20... | collective-permute-start | bytes 6152 | tf_op jit(solution)/shard_map/ppermute | solution.py:608
  38.9 0.8 collective-permute-done
  39.8 2.6 %collective-permute-start.3 = (f32[1,512]{1,0:T(1,128)S(1)}, f32[1,512]{1,0:T(1,128)S(1)}, u32[]{:S(2)}, u32[]{:S(2)}) collective-permute-start(f32[1,512]{1,0:T(1,128)S(1)} %multiply_add_fusion.4.refs_0_), channel_id=1, source_target_pairs={{0,96},{32,64},{64,32},{96,0},{1,97},{33,65},{65,33},{97,1},{2,98}... | collective-permute-start | bytes 6152 | tf_op jit(solution)/shard_map/ppermute | solution.py:608
  42.3 0.5 collective-permute-start.2
  42.9 0.3 collective-permute-start.1
  43.1 0.4 collective-permute-done.3.refs_3_
  43.5 2.8 %collective-permute-done.2.refs_2_ = f32[1,512]{1,0:T(1,128)S(1)} collective-permute-done((f32[1,512]{1,0:T(1,128)S(1)}, f32[1,512]{1,0:T(1,128)S(1)}, u32[]{:S(2)}, u32[]{:S(2)}) %collective-permute-start.2) | collective-permute-done | bytes 2080 | tf_op jit(solution)/shard_map/ppermute | solution.py:608
  46.3 0.6 shard_map.115
  46.9 9.5 %all_to_all.46.refs_0_ = f32[16,8,128]{2,1,0:T(8,128)S(1)} all-to-all(f32[16,8,128]{2,1,0:T(8,128)S(1)} %shard_map.115), channel_id=1, replica_groups=mesh['x'=4,'core'=2,'y'=4,'z'=4] {'y','z'}, dimensions={0} | all-to-all | bytes 131072 | tf_op jit(solution)/shard_map/all_to_all | solution.py:603
  56.4 0.6 shard_map.116
  57.0 10.9 %all_to_all.47.refs_0_ = f32[8,1,512]{2,1,0:T(1,128)S(1)} all-to-all(f32[8,1,512]{2,1,0:T(1,128)S(1)} %shard_map.116), channel_id=1, replica_groups=mesh['x'=4,'core'=2,'y'=4,'z'=4] {'x','core'}, dimensions={0} | all-to-all | bytes 32768 | tf_op jit(solution)/shard_map/all_to_all | solution.py:603
  67.9 0.6 shard_map.117
  68.5 9.5 %all_to_all.48.refs_0_ = f32[16,8,128]{2,1,0:T(8,128)S(1)} all-to-all(f32[16,8,128]{2,1,0:T(8,128)S(1)} %shard_map.117), channel_id=1, replica_groups=mesh['x'=4,'core'=2,'y'=4,'z'=4] {'y','z'}, dimensions={0} | all-to-all | bytes 131072 | tf_op jit(solution)/shard_map/all_to_all | solution.py:603
  78.0 0.6 shard_map.118
  78.6 9.1 %all_to_all.49.refs_0_ = f32[8,1,512]{2,1,0:T(1,128)S(1)} all-to-all(f32[8,1,512]{2,1,0:T(1,128)S(1)} %shard_map.118), channel_id=1, replica_groups=mesh['x'=4,'core'=2,'y'=4,'z'=4] {'x','core'}, dimensions={0} | all-to-all | bytes 32768 | tf_op jit(solution)/shard_map/all_to_all | solution.py:603
  87.7 1.3 shard_map.119
  89.0 3.5 %all-to-all-start.6 = ((f32[16,8,128]{2,1,0:T(8,128)}), f32[16,8,128]{2,1,0:T(8,128)S(1)}, u32[]{:S(2)}, u32[]{:S(2)}) async-start(f32[16,8,128]{2,1,0:T(8,128)} %shard_map.119), calls=%async_computation.6 | async-start | bytes 131072 | tf_op jit(solution)/shard_map/all_to_all | solution.py:603
  92.5 2.4 %plan.1 = (s32[16]{0:T(128)}, s32[64]{0:T(128)}, s32[8]{0:T(128)}, s32[18]{0:T(128)}) custom-call(s32[1]{0:T(128)} %bitcast.row, s32[1]{0:T(128)} %bitcast.1.col, s32[4,1024]{1,0:T(4,128)} %bitcast.21, s32[8,128]{1,0:T(8,128)} %bitcast.24), custom_call_target="tpu_custom_call" | custom-call | tf_op jit(solution)/shard_map/plan/pallas_call | solution.py:645
  94.9 0.6 copy-done.6
  95.5 2.1 %shard_map.121 = bf16[16,272,128]{2,1,0:T(8,128)(2,1)} custom-call(s32[8]{0:T(128)S(1)} %copy-done.6, bf16[2048,128]{1,0:T(8,128)(2,1)} %points.3, f32[8,2,128]{2,1,0:T(2,128)} %bitcast.23), custom_call_target="tpu_custom_call" | custom-call | flops 100000000 | bytes 4194304 | tf_op jit(solution)/shard_map/pallas_call | solution.py:664
  97.6 1.3 all-to-all-done.6.refs_0_
  99.0 5.3 %all-to-all-start.7 = ((bf16[16,272,128]{2,1,0:T(8,128)(2,1)}), bf16[16,272,128]{2,1,0:T(8,128)(2,1)}, u32[]{:S(2)}, u32[]{:S(2)}) async-start(bf16[16,272,128]{2,1,0:T(8,128)(2,1)} %shard_map.121), calls=%async_computation.7 | async-start | bytes 2228224 | tf_op jit(solution)/shard_map/all_to_all | solution.py:603
  104.3 0.6 shard_map.120
  104.9 1.5 collective-permute-start.4
  106.4 0.8 collective-permute-done.4
  107.2 1.0 collective-permute-start.7
  108.2 1.2 collective-permute-start.6
  109.4 1.2 collective-permute-start.5
  110.6 9.9 %all-to-all-done.7.x_hbm = bf16[16,272,128]{2,1,0:T(8,128)(2,1)} async-done(((bf16[16,272,128]{2,1,0:T(8,128)(2,1)}), bf16[16,272,128]{2,1,0:T(8,128)(2,1)}, u32[]{:S(2)}, u32[]{:S(2)}) %all-to-all-start.7) | async-done | bytes 1114144 | tf_op jit(solution)/shard_map/all_to_all | solution.py:603
  120.5 4.4 %shard_map.122 = (f32[16,256,1024]{2,1,0:T(8,128)S(1)}, f32[16,1,256]{2,1,0:T(1,128)S(1)}, f32[16,1,256]{2,1,0:T(1,128)S(1)}) custom-call(s32[16]{0:T(128)S(1)} %copy-done.3, s32[64]{0:T(128)S(1)} %copy-done.4, s32[18]{0:T(128)S(1)} %copy-done.5, f32[64,1,256]{2,1,0:T(1,128)S(1)} %get-tuple-element.36.norms, bf16[16,272,128]{2,1,0:T(8,128)(2,1)} %all-to-all-done.7.x_hbm, ...), custom_call_target="tpu_custom_call" | custom-call | flops 1000000000 | bytes 4194304 | tf_op jit(solution)/shard_map/pallas_call | solution.py:717
  125.0 4.5 %shard_map.123 = (f32[64,1,256]{2,1,0:T(1,128)S(1)}, f32[16,256,1024]{2,1,0:T(8,128)S(1)}) custom-call(s32[1]{0:T(128)} %bitcast.4.base, s32[16]{0:T(128)S(1)} %copy-done.3, s32[64]{0:T(128)S(1)} %copy-done.4, f32[1,512]{1,0:T(1,128)S(1)} %multiply_add_fusion.3.p0, f32[1,512]{1,0:T(1,128)S(1)} %collective-permute-done.5.p1, ...), custom_call_target="tpu_custom_call", output_to_operand_aliasing={{1}: (8, {})} | custom-call | flops 100000000 | bytes 4194304 | tf_op jit(solution)/shard_map/pallas_call | solution.py:738
  129.4 3.5 %collective-permute-start.8 = (f32[64,1,256]{2,1,0:T(1,128)S(1)}, f32[64,1,256]{2,1,0:T(1,128)S(1)}, u32[]{:S(2)}, u32[]{:S(2)}) collective-permute-start(f32[64,1,256]{2,1,0:T(1,128)S(1)} %get-tuple-element.38), channel_id=1, source_target_pairs={{0,16},{16,0},{1,17},{17,1},{2,18},{18,2},{3,19},{19,3},{4,20},{20... | collective-permute-start | bytes 196616 | tf_op jit(solution)/shard_map/ppermute | solution.py:608
  132.9 0.9 collective-permute-done.8
  134.1 0.8 collective-permute-start.11
  134.9 1.2 collective-permute-start.10
  136.1 1.3 collective-permute-start.9
  137.4 1.1 collective-permute-done.11.l3
  138.5 1.1 collective-permute-done.10.l2
  139.6 0.8 collective-permute-done.9.l1
  140.4 6.6 %shard_map.124 = (f32[64,1,256]{2,1,0:T(1,128)S(1)}, f32[64,1,256]{2,1,0:T(1,128)S(1)}, f32[16,1,256]{2,1,0:T(1,128)S(1)}, f32[16,256,1024]{2,1,0:T(8,128)S(1)}) custom-call(s32[16]{0:T(128)S(1)} %copy-done.3, s32[64]{0:T(128)S(1)} %copy-done.4, f32[64,1,256]{2,1,0:T(1,128)S(1)} %multiply_add_fusion.2.l0, ...), custom_call_target="tpu_custom_call", output_to_operand_aliasing={{3}: (7, {})} | custom-call | flops 100000000 | bytes 4194304 | tf_op jit(solution)/shard_map/pallas_call | solution.py:754
  147.0 1.6 collective-permute-start.12
  148.6 0.8 collective-permute-done.12
  149.5 0.4 collective-permute-done.16
  149.8 0.4 multiply_add_fusion
  150.3 1.8 %collective-permute-start.15 = (f32[64,1,256]{2,1,0:T(1,128)S(1)}, f32[64,1,256]{2,1,0:T(1,128)S(1)}, u32[]{:S(2)}, u32[]{:S(2)}) collective-permute-start(f32[64,1,256]{2,1,0:T(1,128)S(1)} %get-tuple-element.51.l0), channel_id=1, source_target_pairs={{0,96},{32,64},{64,32},{96,0},{1,97},{33,65},{65,33},{97,1},{2,98}... | collective-permute-start | bytes 196616 | tf_op jit(solution)/shard_map/ppermute | solution.py:608
  152.0 0.8 collective-permute-start.14
  152.9 0.7 collective-permute-start.13
  153.6 1.7 collective-permute-start.19
  155.3 0.8 collective-permute-start.18
  156.1 0.7 collective-permute-start.17
  156.9 4.9 %shard_map.125 = (f32[64,1,256]{2,1,0:T(1,128)}, f32[16,1,512]{2,1,0:T(1,128)}) custom-call(s32[16]{0:T(128)S(1)} %copy-done.3, s32[64]{0:T(128)S(1)} %copy-done.4, s32[18]{0:T(128)S(1)} %copy-done.5, f32[64,1,256]{2,1,0:T(1,128)S(1)} %get-tuple-element.51.l0, f32[64,1,256]{2,1,0:T(1,128)S(1)} %collective-permute-done.13.l1, ...), custom_call_target="tpu_custom_call" | custom-call | flops 100000000 | bytes 4194304 | tf_op jit(solution)/shard_map/pallas_call | solution.py:768
  161.8 3.5 %all-to-all-start.8 = ((f32[16,1,512]{2,1,0:T(1,128)}), f32[16,1,512]{2,1,0:T(1,128)S(1)}, u32[]{:S(2)}, u32[]{:S(2)}) async-start(f32[16,1,512]{2,1,0:T(1,128)} %get-tuple-element.45), calls=%async_computation.8 | async-start | bytes 65536 | tf_op jit(solution)/shard_map/all_to_all | solution.py:603
  165.3 1.5 add_add_fusion
  166.8 4.9 %all-to-all-done.8.back = f32[16,1,512]{2,1,0:T(1,128)S(1)} async-done(((f32[16,1,512]{2,1,0:T(1,128)}), f32[16,1,512]{2,1,0:T(1,128)S(1)}, u32[]{:S(2)}, u32[]{:S(2)}) %all-to-all-start.8) | async-done | bytes 32800 | tf_op jit(solution)/shard_map/all_to_all | solution.py:603
  171.7 1.2 shard_map.126
  (28 shorter events, 0.5 us)
Async XLA Ops:
  2.8 19.6 %all-to-all-start = ((f32[16,72,128]{2,1,0:T(8,128)}), f32[16,72,128]{2,1,0:T(8,128)S(1)}, u32[]{:S(2)}, u32[]{:S(2)}) async-start(f32[16,72,128]{2,1,0:T(8,128)} %shard_map.111), calls=%async_computation | async-start | bytes 1179648 | tf_op jit(solution)/shard_map/all_to_all | solution.py:603
  12.4 0.8 copy-start
  36.2 3.6 %collective-permute-start = (f32[1,512]{1,0:T(1,128)S(1)}, f32[1,512]{1,0:T(1,128)S(1)}, u32[]{:S(2)}, u32[]{:S(2)}) collective-permute-start(f32[1,512]{1,0:T(1,128)S(1)} %shard_map.114), channel_id=1, source_target_pairs={{0,16},{16,0},{1,17},{17,1},{2,18},{18,2},{3,19},{19,3},{4,20},{20... | collective-permute-start | bytes 6152 | tf_op jit(solution)/shard_map/ppermute | solution.py:608
  39.8 3.7 %collective-permute-start.3 = (f32[1,512]{1,0:T(1,128)S(1)}, f32[1,512]{1,0:T(1,128)S(1)}, u32[]{:S(2)}, u32[]{:S(2)}) collective-permute-start(f32[1,512]{1,0:T(1,128)S(1)} %multiply_add_fusion.4.refs_0_), channel_id=1, source_target_pairs={{0,96},{32,64},{64,32},{96,0},{1,97},{33,65},{65,33},{97,1},{2,98}... | collective-permute-start | bytes 6152 | tf_op jit(solution)/shard_map/ppermute | solution.py:608
  42.3 3.9 %collective-permute-start.2 = (f32[1,512]{1,0:T(1,128)S(1)}, f32[1,512]{1,0:T(1,128)S(1)}, u32[]{:S(2)}, u32[]{:S(2)}) collective-permute-start(f32[1,512]{1,0:T(1,128)S(1)} %multiply_add_fusion.4.refs_0_), channel_id=1, source_target_pairs={{0,64},{32,96},{64,0},{96,32},{1,65},{33,97},{65,1},{97,33},{2,66}... | collective-permute-start | bytes 6152 | tf_op jit(solution)/shard_map/ppermute | solution.py:608
  42.9 3.4 %collective-permute-start.1 = (f32[1,512]{1,0:T(1,128)S(1)}, f32[1,512]{1,0:T(1,128)S(1)}, u32[]{:S(2)}, u32[]{:S(2)}) collective-permute-start(f32[1,512]{1,0:T(1,128)S(1)} %multiply_add_fusion.4.refs_0_), channel_id=1, source_target_pairs={{0,32},{32,0},{64,96},{96,64},{1,33},{33,1},{65,97},{97,65},{2,34}... | collective-permute-start | bytes 6152 | tf_op jit(solution)/shard_map/ppermute | solution.py:608
  89.0 10.0 %all-to-all-start.6 = ((f32[16,8,128]{2,1,0:T(8,128)}), f32[16,8,128]{2,1,0:T(8,128)S(1)}, u32[]{:S(2)}, u32[]{:S(2)}) async-start(f32[16,8,128]{2,1,0:T(8,128)} %shard_map.119), calls=%async_computation.6 | async-start | bytes 131072 | tf_op jit(solution)/shard_map/all_to_all | solution.py:603
  94.9 25.6 %copy-start.3 = (s32[16]{0:T(128)S(1)}, s32[16]{0:T(128)}, u32[]{:S(2)}) copy-start(s32[16]{0:T(128)} %get-tuple-element.28.counts) | copy-start | bytes 196
  94.9 25.6 %copy-start.4 = (s32[64]{0:T(128)S(1)}, s32[64]{0:T(128)}, u32[]{:S(2)}) copy-start(s32[64]{0:T(128)} %get-tuple-element.29.blocks) | copy-start | bytes 772
  94.9 25.6 %copy-start.5 = (s32[18]{0:T(128)S(1)}, s32[18]{0:T(128)}, u32[]{:S(2)}) copy-start(s32[18]{0:T(128)} %get-tuple-element.30.order) | copy-start | bytes 220
  94.9 0.6 copy-start.6
  99.0 21.5 %all-to-all-start.7 = ((bf16[16,272,128]{2,1,0:T(8,128)(2,1)}), bf16[16,272,128]{2,1,0:T(8,128)(2,1)}, u32[]{:S(2)}, u32[]{:S(2)}) async-start(bf16[16,272,128]{2,1,0:T(8,128)(2,1)} %shard_map.121), calls=%async_computation.7 | async-start | bytes 2228224 | tf_op jit(solution)/shard_map/all_to_all | solution.py:603
  104.3 20.7 %copy-start.1 = (s32[16384]{0:T(1024)S(1)}, s32[16384]{0:T(1024)}, u32[]{:S(2)}) copy-start(s32[16384]{0:T(1024)} %param.11) | copy-start | bytes 196612
  104.9 2.4 %collective-permute-start.4 = (f32[1,512]{1,0:T(1,128)S(1)}, f32[1,512]{1,0:T(1,128)S(1)}, u32[]{:S(2)}, u32[]{:S(2)}) collective-permute-start(f32[1,512]{1,0:T(1,128)S(1)} %shard_map.120), channel_id=1, source_target_pairs={{0,16},{16,0},{1,17},{17,1},{2,18},{18,2},{3,19},{19,3},{4,20},{20... | collective-permute-start | bytes 6152 | tf_op jit(solution)/shard_map/ppermute | solution.py:608
  107.2 17.7 %collective-permute-start.7 = (f32[1,512]{1,0:T(1,128)S(1)}, f32[1,512]{1,0:T(1,128)S(1)}, u32[]{:S(2)}, u32[]{:S(2)}) collective-permute-start(f32[1,512]{1,0:T(1,128)S(1)} %multiply_add_fusion.3.p0), channel_id=1, source_target_pairs={{0,96},{32,64},{64,32},{96,0},{1,97},{33,65},{65,33},{97,1},{2,98}... | collective-permute-start | bytes 6152 | tf_op jit(solution)/shard_map/ppermute | solution.py:608
  108.2 16.7 %collective-permute-start.6 = (f32[1,512]{1,0:T(1,128)S(1)}, f32[1,512]{1,0:T(1,128)S(1)}, u32[]{:S(2)}, u32[]{:S(2)}) collective-permute-start(f32[1,512]{1,0:T(1,128)S(1)} %multiply_add_fusion.3.p0), channel_id=1, source_target_pairs={{0,64},{32,96},{64,0},{96,32},{1,65},{33,97},{65,1},{97,33},{2,66}... | collective-permute-start | bytes 6152 | tf_op jit(solution)/shard_map/ppermute | solution.py:608
  109.4 15.5 %collective-permute-start.5 = (f32[1,512]{1,0:T(1,128)S(1)}, f32[1,512]{1,0:T(1,128)S(1)}, u32[]{:S(2)}, u32[]{:S(2)}) collective-permute-start(f32[1,512]{1,0:T(1,128)S(1)} %multiply_add_fusion.3.p0), channel_id=1, source_target_pairs={{0,32},{32,0},{64,96},{96,64},{1,33},{33,1},{65,97},{97,65},{2,34}... | collective-permute-start | bytes 6152 | tf_op jit(solution)/shard_map/ppermute | solution.py:608
  129.4 4.4 %collective-permute-start.8 = (f32[64,1,256]{2,1,0:T(1,128)S(1)}, f32[64,1,256]{2,1,0:T(1,128)S(1)}, u32[]{:S(2)}, u32[]{:S(2)}) collective-permute-start(f32[64,1,256]{2,1,0:T(1,128)S(1)} %get-tuple-element.38), channel_id=1, source_target_pairs={{0,16},{16,0},{1,17},{17,1},{2,18},{18,2},{3,19},{19,3},{4,20},{20... | collective-permute-start | bytes 196616 | tf_op jit(solution)/shard_map/ppermute | solution.py:608
  134.1 4.4 %collective-permute-start.11 = (f32[64,1,256]{2,1,0:T(1,128)S(1)}, f32[64,1,256]{2,1,0:T(1,128)S(1)}, u32[]{:S(2)}, u32[]{:S(2)}) collective-permute-start(f32[64,1,256]{2,1,0:T(1,128)S(1)} %multiply_add_fusion.2.l0), channel_id=1, source_target_pairs={{0,96},{32,64},{64,32},{96,0},{1,97},{33,65},{65,33},{97,1},{2,98}... | collective-permute-start | bytes 196616 | tf_op jit(solution)/shard_map/ppermute | solution.py:608
  134.9 4.7 %collective-permute-start.10 = (f32[64,1,256]{2,1,0:T(1,128)S(1)}, f32[64,1,256]{2,1,0:T(1,128)S(1)}, u32[]{:S(2)}, u32[]{:S(2)}) collective-permute-start(f32[64,1,256]{2,1,0:T(1,128)S(1)} %multiply_add_fusion.2.l0), channel_id=1, source_target_pairs={{0,64},{32,96},{64,0},{96,32},{1,65},{33,97},{65,1},{97,33},{2,66}... | collective-permute-start | bytes 196616 | tf_op jit(solution)/shard_map/ppermute | solution.py:608
  136.1 4.3 %collective-permute-start.9 = (f32[64,1,256]{2,1,0:T(1,128)S(1)}, f32[64,1,256]{2,1,0:T(1,128)S(1)}, u32[]{:S(2)}, u32[]{:S(2)}) collective-permute-start(f32[64,1,256]{2,1,0:T(1,128)S(1)} %multiply_add_fusion.2.l0), channel_id=1, source_target_pairs={{0,32},{32,0},{64,96},{96,64},{1,33},{33,1},{65,97},{97,65},{2,34}... | collective-permute-start | bytes 196616 | tf_op jit(solution)/shard_map/ppermute | solution.py:608
  140.4 16.5 %copy-start.2 = (f32[16384]{0:T(1024)S(1)}, f32[16384]{0:T(1024)}, u32[]{:S(2)}) copy-start(f32[16384]{0:T(1024)} %param.15) | copy-start | bytes 196612
  147.0 2.5 %collective-permute-start.12 = (f32[64,1,256]{2,1,0:T(1,128)S(1)}, f32[64,1,256]{2,1,0:T(1,128)S(1)}, u32[]{:S(2)}, u32[]{:S(2)}) collective-permute-start(f32[64,1,256]{2,1,0:T(1,128)S(1)} %get-tuple-element.41), channel_id=1, source_target_pairs={{0,16},{16,0},{1,17},{17,1},{2,18},{18,2},{3,19},{19,3},{4,20},{20... | collective-permute-start | bytes 196616 | tf_op jit(solution)/shard_map/ppermute | solution.py:608
  148.6 1.3 collective-permute-start.16
  150.3 5.9 %collective-permute-start.15 = (f32[64,1,256]{2,1,0:T(1,128)S(1)}, f32[64,1,256]{2,1,0:T(1,128)S(1)}, u32[]{:S(2)}, u32[]{:S(2)}) collective-permute-start(f32[64,1,256]{2,1,0:T(1,128)S(1)} %get-tuple-element.51.l0), channel_id=1, source_target_pairs={{0,96},{32,64},{64,32},{96,0},{1,97},{33,65},{65,33},{97,1},{2,98}... | collective-permute-start | bytes 196616 | tf_op jit(solution)/shard_map/ppermute | solution.py:608
  152.0 4.8 %collective-permute-start.14 = (f32[64,1,256]{2,1,0:T(1,128)S(1)}, f32[64,1,256]{2,1,0:T(1,128)S(1)}, u32[]{:S(2)}, u32[]{:S(2)}) collective-permute-start(f32[64,1,256]{2,1,0:T(1,128)S(1)} %get-tuple-element.51.l0), channel_id=1, source_target_pairs={{0,64},{32,96},{64,0},{96,32},{1,65},{33,97},{65,1},{97,33},{2,66}... | collective-permute-start | bytes 196616 | tf_op jit(solution)/shard_map/ppermute | solution.py:608
  152.9 4.0 %collective-permute-start.13 = (f32[64,1,256]{2,1,0:T(1,128)S(1)}, f32[64,1,256]{2,1,0:T(1,128)S(1)}, u32[]{:S(2)}, u32[]{:S(2)}) collective-permute-start(f32[64,1,256]{2,1,0:T(1,128)S(1)} %get-tuple-element.51.l0), channel_id=1, source_target_pairs={{0,32},{32,0},{64,96},{96,64},{1,33},{33,1},{65,97},{97,65},{2,34}... | collective-permute-start | bytes 196616 | tf_op jit(solution)/shard_map/ppermute | solution.py:608
  153.6 11.7 %collective-permute-start.19 = (f32[64,1,256]{2,1,0:T(1,128)S(1)}, f32[64,1,256]{2,1,0:T(1,128)S(1)}, u32[]{:S(2)}, u32[]{:S(2)}) collective-permute-start(f32[64,1,256]{2,1,0:T(1,128)S(1)} %get-tuple-element.50), channel_id=1, source_target_pairs={{0,96},{32,64},{64,32},{96,0},{1,97},{33,65},{65,33},{97,1},{2,98}... | collective-permute-start | bytes 196616 | tf_op jit(solution)/shard_map/ppermute | solution.py:608
  155.3 10.0 %collective-permute-start.18 = (f32[64,1,256]{2,1,0:T(1,128)S(1)}, f32[64,1,256]{2,1,0:T(1,128)S(1)}, u32[]{:S(2)}, u32[]{:S(2)}) collective-permute-start(f32[64,1,256]{2,1,0:T(1,128)S(1)} %get-tuple-element.50), channel_id=1, source_target_pairs={{0,64},{32,96},{64,0},{96,32},{1,65},{33,97},{65,1},{97,33},{2,66}... | collective-permute-start | bytes 196616 | tf_op jit(solution)/shard_map/ppermute | solution.py:608
  156.1 9.1 %collective-permute-start.17 = (f32[64,1,256]{2,1,0:T(1,128)S(1)}, f32[64,1,256]{2,1,0:T(1,128)S(1)}, u32[]{:S(2)}, u32[]{:S(2)}) collective-permute-start(f32[64,1,256]{2,1,0:T(1,128)S(1)} %get-tuple-element.50), channel_id=1, source_target_pairs={{0,32},{32,0},{64,96},{96,64},{1,33},{33,1},{65,97},{97,65},{2,34}... | collective-permute-start | bytes 196616 | tf_op jit(solution)/shard_map/ppermute | solution.py:608
  156.9 14.8 %copy-start.7 = (s32[8]{0:T(128)S(1)}, s32[8]{0:T(128)}, u32[]{:S(2)}) copy-start(s32[8]{0:T(128)} %get-tuple-element.27.owners) | copy-start | bytes 100
  161.8 9.9 %all-to-all-start.8 = ((f32[16,1,512]{2,1,0:T(1,128)}), f32[16,1,512]{2,1,0:T(1,128)S(1)}, u32[]{:S(2)}, u32[]{:S(2)}) async-start(f32[16,1,512]{2,1,0:T(1,128)} %get-tuple-element.45), calls=%async_computation.8 | async-start | bytes 65536 | tf_op jit(solution)/shard_map/all_to_all | solution.py:603
